TPU v7x, 32 devices: a 4x4x1 block of a 4x4x8 slice. The times are simulated.
32 devices in a mesh: dp: 1 (over z), cp: 32 (over y, x, core).
Axes of the slice: x: 4, y: 4, z: 1, core: 2. Of those that a mesh axis runs over, the one named last changes fastest.
The devices are a block of a 4x4x8 slice.
Arguments:
- hidden: bfloat16 [6, 4096, 4096], P('dp', 'cp')
- positions: int32 [6, 4096], P('dp', 'cp')
- norm_gain: bfloat16 [4096], replicated
- w_query: bfloat16 [4096, 4096], replicated
- w_key: bfloat16 [4096, 1024], replicated
- w_value: bfloat16 [4096, 1024], replicated
- w_out: bfloat16 [32, 128, 4096], replicated
Outputs:
- output: bfloat16 [6, 4096, 4096], P('dp', 'cp')
All inputs are finite; a program needn't handle non-finite values.
Results may differ from a plain program's by a relative error of at most 0.00731925.
Values are sent between devices in bfloat16 or wider.
A program may use at most 768 MiB of HBM per device.

v0:
```python
import jax
import jax.numpy as jnp
from jax import lax
from jax.sharding import PartitionSpec as P


def rms_norm(hidden, norm_gain):
    x_f32 = hidden.astype(jnp.float32)
    inv_rms = lax.rsqrt(jnp.mean(x_f32 * x_f32, axis=-1, keepdims=True) + 1e-5)
    return (x_f32 * inv_rms * norm_gain.astype(jnp.float32)).astype(jnp.bfloat16)


def rotary(proj_f32, positions):
    head_dim = proj_f32.shape[-1]
    half_dim = head_dim // 2
    inv_freq = 10000.0 ** (-2.0 * jnp.arange(half_dim, dtype=jnp.float32) / head_dim)
    angles = positions.astype(jnp.float32)[:, :, None] * inv_freq
    cos_part = jnp.cos(angles)[:, :, None, :]
    sin_part = jnp.sin(angles)[:, :, None, :]
    first_half = proj_f32[..., :half_dim]
    second_half = proj_f32[..., half_dim:]
    return jnp.concatenate([first_half * cos_part - second_half * sin_part, second_half * cos_part + first_half * sin_part], axis=-1).astype(jnp.bfloat16)


def attend_block(q_grp, k_blk, v_blk, att_state, allowed):
    run_max, run_sum, acc_out = att_state
    scores = jnp.einsum('bqkgd,bskd->bkgqs', q_grp, k_blk, preferred_element_type=jnp.float32) * (q_grp.shape[-1] ** -0.5)
    if allowed is not None:
        scores = jnp.where(allowed, scores, -jnp.inf)
    new_max = jnp.maximum(run_max, jnp.max(scores, axis=-1))
    prob_blk = jnp.exp(scores - new_max[..., None])
    rescale = jnp.exp(run_max - new_max)
    new_sum = run_sum * rescale + jnp.sum(prob_blk, axis=-1)
    new_acc = acc_out * rescale[..., None] + jnp.einsum('bkgqs,bskd->bkgqd', prob_blk, v_blk, preferred_element_type=jnp.float32)
    return new_max, new_sum, new_acc


def solution(mesh):
    n_cp = mesh.shape['cp']
    shift_pairs = [(src_dev, (src_dev + 1) % n_cp) for src_dev in range(n_cp)]

    def local_block(hidden, positions, norm_gain, w_query, w_key, w_value, w_out):
        batch_loc, seq_loc, model_dim = hidden.shape
        n_heads, head_dim, _ = w_out.shape
        n_kv = w_key.shape[1] // head_dim
        n_groups = n_heads // n_kv
        normed = rms_norm(hidden, norm_gain)
        q_rot = rotary(jnp.einsum('bsd,de->bse', normed, w_query, preferred_element_type=jnp.float32).reshape(batch_loc, seq_loc, n_heads, head_dim), positions)
        k_rot = rotary(jnp.einsum('bsd,de->bse', normed, w_key, preferred_element_type=jnp.float32).reshape(batch_loc, seq_loc, n_kv, head_dim), positions)
        v_loc = jnp.einsum('bsd,de->bse', normed, w_value, preferred_element_type=jnp.float32).astype(jnp.bfloat16).reshape(batch_loc, seq_loc, n_kv, head_dim)
        q_grp = q_rot.reshape(batch_loc, seq_loc, n_kv, n_groups, head_dim)
        my_index = lax.axis_index('cp')
        token_idx = jnp.arange(seq_loc)
        diag_mask = token_idx[:, None] >= token_idx[None, :]
        start_state = (
            jnp.full((batch_loc, n_kv, n_groups, seq_loc), -jnp.inf, jnp.float32),
            jnp.zeros((batch_loc, n_kv, n_groups, seq_loc), jnp.float32),
            jnp.zeros((batch_loc, n_kv, n_groups, seq_loc, head_dim), jnp.float32),
        )
        att_state = attend_block(q_grp, k_rot, v_loc, start_state, diag_mask)

        def step_fn(step_idx, loop_state):
            k_blk, v_blk, att_prev = loop_state
            k_blk, v_blk = lax.ppermute((k_blk, v_blk), 'cp', shift_pairs)
            src_block = (my_index - step_idx) % n_cp
            att_next = lax.cond(src_block < my_index, lambda state_kept: attend_block(q_grp, k_blk, v_blk, state_kept, None), lambda state_kept: state_kept, att_prev)
            return k_blk, v_blk, att_next

        _, _, final_state = lax.fori_loop(1, n_cp, step_fn, (k_rot, v_loc, att_state))
        run_max, run_sum, acc_out = final_state
        attn_out = (acc_out / run_sum[..., None]).astype(jnp.bfloat16)
        proj_out = jnp.einsum('bkgqd,kgde->bqe', attn_out, w_out.reshape(n_kv, n_groups, head_dim, model_dim), preferred_element_type=jnp.float32)
        return (hidden.astype(jnp.float32) + proj_out).astype(jnp.bfloat16)

    act_spec = P('dp', 'cp', None)
    return jax.shard_map(local_block, mesh=mesh, in_specs=(act_spec, P('dp', 'cp'), P(), P(), P(), P(), P()), out_specs=act_spec, check_vma=False)
```

profile of v0, /device:TPU:126, one launch (start us, length us, event | category | flops | bytes accessed | tf_op | source)
XLA Modules:
  0.0 2066.4 jit_solution(10516110721118267145)
XLA Ops:
  22.6 32.3 %fusion.12 = f32[6,128,4096]{2,1,0:T(8,128)} fusion(bf16[4096,4096]{1,0:T(8,128)(2,1)} %param.14, bf16[6,128,4096]{2,1,0:T(8,128)(2,1)S(1)} %bitcast.110, f32[4096]{0:T(1024)S(1)} %convert_element_type.37, f32[6,128]{1,0:T(8,128)S(1)} %add_rsqrt_fusion), kind=kOutput, calls=%fused_computation.14 | convolution fusion | flops 25782386688 | bytes 52448256 | tf_op jit(solution)/shard_map/bsd,de->bse/dot_general | solution.py:48
  119.1 1908.5 %while.23 = (s32[]{:T(128)}, bf16[6,128,8,128]{3,1,2,0:T(8,128)(2,1)}, bf16[6,128,8,128]{3,1,2,0:T(8,128)(2,1)}, f32[6,8,4,128]{3,2,1,0:T(4,128)S(1)}, f32[6,8,4...) while((s32[]{:T(128)}, ...), condition=%wide.region_8.9_spmd, body=%wide.region_3.8_spmd.sunk | while | flops 1638973440 | bytes 92799400 | solution.py:69
  119.8 19.7 collective-permute-done
  156.3 23.2 %conditional.2 = ((f32[6,8,4,128]{3,2,1,0:T(4,128)S(1)}, f32[6,8,4,128]{3,2,1,0:T(4,128)S(1)}, f32[6,8,4,128,128]{4,3,2,1,0:T(8,128)})) conditional(s32[]{:T(128)} %convert_element_type.74, (f32[6,8,4,128]{3,2,1,0:T(4,128)S(1)}, f32[6,8,4,128]{3,2,1,0:T(4,128)S(1)}, f32[6,8,4,128,128]{4,3,2,1,0:T(8,128)}) %tuple.55, ...), branch_computations={%region_4.4_spmd, %region_5.7_spmd} | conditional | flops 1638973440 | bytes 73924640 | solution.py:66
  181.9 19.8 collective-permute-done
  218.6 23.2 %conditional.2 = ((f32[6,8,4,128]{3,2,1,0:T(4,128)S(1)}, f32[6,8,4,128]{3,2,1,0:T(4,128)S(1)}, f32[6,8,4,128,128]{4,3,2,1,0:T(8,128)})) conditional(s32[]{:T(128)} %convert_element_type.74, (f32[6,8,4,128]{3,2,1,0:T(4,128)S(1)}, f32[6,8,4,128]{3,2,1,0:T(4,128)S(1)}, f32[6,8,4,128,128]{4,3,2,1,0:T(8,128)}) %tuple.55, ...), branch_computations={%region_4.4_spmd, %region_5.7_spmd} | conditional | flops 1638973440 | bytes 73924640 | solution.py:66
  244.2 19.8 collective-permute-done
  280.9 23.2 %conditional.2 = ((f32[6,8,4,128]{3,2,1,0:T(4,128)S(1)}, f32[6,8,4,128]{3,2,1,0:T(4,128)S(1)}, f32[6,8,4,128,128]{4,3,2,1,0:T(8,128)})) conditional(s32[]{:T(128)} %convert_element_type.74, (f32[6,8,4,128]{3,2,1,0:T(4,128)S(1)}, f32[6,8,4,128]{3,2,1,0:T(4,128)S(1)}, f32[6,8,4,128,128]{4,3,2,1,0:T(8,128)}) %tuple.55, ...), branch_computations={%region_4.4_spmd, %region_5.7_spmd} | conditional | flops 1638973440 | bytes 73924640 | solution.py:66
  306.5 19.8 collective-permute-done
  343.2 23.2 %conditional.2 = ((f32[6,8,4,128]{3,2,1,0:T(4,128)S(1)}, f32[6,8,4,128]{3,2,1,0:T(4,128)S(1)}, f32[6,8,4,128,128]{4,3,2,1,0:T(8,128)})) conditional(s32[]{:T(128)} %convert_element_type.74, (f32[6,8,4,128]{3,2,1,0:T(4,128)S(1)}, f32[6,8,4,128]{3,2,1,0:T(4,128)S(1)}, f32[6,8,4,128,128]{4,3,2,1,0:T(8,128)}) %tuple.55, ...), branch_computations={%region_4.4_spmd, %region_5.7_spmd} | conditional | flops 1638973440 | bytes 73924640 | solution.py:66
  368.8 19.8 collective-permute-done
  405.5 23.2 %conditional.2 = ((f32[6,8,4,128]{3,2,1,0:T(4,128)S(1)}, f32[6,8,4,128]{3,2,1,0:T(4,128)S(1)}, f32[6,8,4,128,128]{4,3,2,1,0:T(8,128)})) conditional(s32[]{:T(128)} %convert_element_type.74, (f32[6,8,4,128]{3,2,1,0:T(4,128)S(1)}, f32[6,8,4,128]{3,2,1,0:T(4,128)S(1)}, f32[6,8,4,128,128]{4,3,2,1,0:T(8,128)}) %tuple.55, ...), branch_computations={%region_4.4_spmd, %region_5.7_spmd} | conditional | flops 1638973440 | bytes 73924640 | solution.py:66
  431.1 19.8 collective-permute-done
  467.8 23.2 %conditional.2 = ((f32[6,8,4,128]{3,2,1,0:T(4,128)S(1)}, f32[6,8,4,128]{3,2,1,0:T(4,128)S(1)}, f32[6,8,4,128,128]{4,3,2,1,0:T(8,128)})) conditional(s32[]{:T(128)} %convert_element_type.74, (f32[6,8,4,128]{3,2,1,0:T(4,128)S(1)}, f32[6,8,4,128]{3,2,1,0:T(4,128)S(1)}, f32[6,8,4,128,128]{4,3,2,1,0:T(8,128)}) %tuple.55, ...), branch_computations={%region_4.4_spmd, %region_5.7_spmd} | conditional | flops 1638973440 | bytes 73924640 | solution.py:66
  493.4 19.8 collective-permute-done
  530.1 23.2 %conditional.2 = ((f32[6,8,4,128]{3,2,1,0:T(4,128)S(1)}, f32[6,8,4,128]{3,2,1,0:T(4,128)S(1)}, f32[6,8,4,128,128]{4,3,2,1,0:T(8,128)})) conditional(s32[]{:T(128)} %convert_element_type.74, (f32[6,8,4,128]{3,2,1,0:T(4,128)S(1)}, f32[6,8,4,128]{3,2,1,0:T(4,128)S(1)}, f32[6,8,4,128,128]{4,3,2,1,0:T(8,128)}) %tuple.55, ...), branch_computations={%region_4.4_spmd, %region_5.7_spmd} | conditional | flops 1638973440 | bytes 73924640 | solution.py:66
  555.7 19.8 collective-permute-done
  592.4 23.2 %conditional.2 = ((f32[6,8,4,128]{3,2,1,0:T(4,128)S(1)}, f32[6,8,4,128]{3,2,1,0:T(4,128)S(1)}, f32[6,8,4,128,128]{4,3,2,1,0:T(8,128)})) conditional(s32[]{:T(128)} %convert_element_type.74, (f32[6,8,4,128]{3,2,1,0:T(4,128)S(1)}, f32[6,8,4,128]{3,2,1,0:T(4,128)S(1)}, f32[6,8,4,128,128]{4,3,2,1,0:T(8,128)}) %tuple.55, ...), branch_computations={%region_4.4_spmd, %region_5.7_spmd} | conditional | flops 1638973440 | bytes 73924640 | solution.py:66
  618.0 19.8 collective-permute-done
  654.7 23.2 %conditional.2 = ((f32[6,8,4,128]{3,2,1,0:T(4,128)S(1)}, f32[6,8,4,128]{3,2,1,0:T(4,128)S(1)}, f32[6,8,4,128,128]{4,3,2,1,0:T(8,128)})) conditional(s32[]{:T(128)} %convert_element_type.74, (f32[6,8,4,128]{3,2,1,0:T(4,128)S(1)}, f32[6,8,4,128]{3,2,1,0:T(4,128)S(1)}, f32[6,8,4,128,128]{4,3,2,1,0:T(8,128)}) %tuple.55, ...), branch_computations={%region_4.4_spmd, %region_5.7_spmd} | conditional | flops 1638973440 | bytes 73924640 | solution.py:66
  680.3 19.8 collective-permute-done
  717.0 23.2 %conditional.2 = ((f32[6,8,4,128]{3,2,1,0:T(4,128)S(1)}, f32[6,8,4,128]{3,2,1,0:T(4,128)S(1)}, f32[6,8,4,128,128]{4,3,2,1,0:T(8,128)})) conditional(s32[]{:T(128)} %convert_element_type.74, (f32[6,8,4,128]{3,2,1,0:T(4,128)S(1)}, f32[6,8,4,128]{3,2,1,0:T(4,128)S(1)}, f32[6,8,4,128,128]{4,3,2,1,0:T(8,128)}) %tuple.55, ...), branch_computations={%region_4.4_spmd, %region_5.7_spmd} | conditional | flops 1638973440 | bytes 73924640 | solution.py:66
  742.6 19.8 collective-permute-done
  779.2 23.2 %conditional.2 = ((f32[6,8,4,128]{3,2,1,0:T(4,128)S(1)}, f32[6,8,4,128]{3,2,1,0:T(4,128)S(1)}, f32[6,8,4,128,128]{4,3,2,1,0:T(8,128)})) conditional(s32[]{:T(128)} %convert_element_type.74, (f32[6,8,4,128]{3,2,1,0:T(4,128)S(1)}, f32[6,8,4,128]{3,2,1,0:T(4,128)S(1)}, f32[6,8,4,128,128]{4,3,2,1,0:T(8,128)}) %tuple.55, ...), branch_computations={%region_4.4_spmd, %region_5.7_spmd} | conditional | flops 1638973440 | bytes 73924640 | solution.py:66
  804.9 19.8 collective-permute-done
  841.5 23.2 %conditional.2 = ((f32[6,8,4,128]{3,2,1,0:T(4,128)S(1)}, f32[6,8,4,128]{3,2,1,0:T(4,128)S(1)}, f32[6,8,4,128,128]{4,3,2,1,0:T(8,128)})) conditional(s32[]{:T(128)} %convert_element_type.74, (f32[6,8,4,128]{3,2,1,0:T(4,128)S(1)}, f32[6,8,4,128]{3,2,1,0:T(4,128)S(1)}, f32[6,8,4,128,128]{4,3,2,1,0:T(8,128)}) %tuple.55, ...), branch_computations={%region_4.4_spmd, %region_5.7_spmd} | conditional | flops 1638973440 | bytes 73924640 | solution.py:66
  867.1 19.8 collective-permute-done
  903.8 23.2 %conditional.2 = ((f32[6,8,4,128]{3,2,1,0:T(4,128)S(1)}, f32[6,8,4,128]{3,2,1,0:T(4,128)S(1)}, f32[6,8,4,128,128]{4,3,2,1,0:T(8,128)})) conditional(s32[]{:T(128)} %convert_element_type.74, (f32[6,8,4,128]{3,2,1,0:T(4,128)S(1)}, f32[6,8,4,128]{3,2,1,0:T(4,128)S(1)}, f32[6,8,4,128,128]{4,3,2,1,0:T(8,128)}) %tuple.55, ...), branch_computations={%region_4.4_spmd, %region_5.7_spmd} | conditional | flops 1638973440 | bytes 73924640 | solution.py:66
  929.4 19.8 collective-permute-done
  966.1 23.2 %conditional.2 = ((f32[6,8,4,128]{3,2,1,0:T(4,128)S(1)}, f32[6,8,4,128]{3,2,1,0:T(4,128)S(1)}, f32[6,8,4,128,128]{4,3,2,1,0:T(8,128)})) conditional(s32[]{:T(128)} %convert_element_type.74, (f32[6,8,4,128]{3,2,1,0:T(4,128)S(1)}, f32[6,8,4,128]{3,2,1,0:T(4,128)S(1)}, f32[6,8,4,128,128]{4,3,2,1,0:T(8,128)}) %tuple.55, ...), branch_computations={%region_4.4_spmd, %region_5.7_spmd} | conditional | flops 1638973440 | bytes 73924640 | solution.py:66
  991.7 19.8 collective-permute-done
  1028.4 23.2 %conditional.2 = ((f32[6,8,4,128]{3,2,1,0:T(4,128)S(1)}, f32[6,8,4,128]{3,2,1,0:T(4,128)S(1)}, f32[6,8,4,128,128]{4,3,2,1,0:T(8,128)})) conditional(s32[]{:T(128)} %convert_element_type.74, (f32[6,8,4,128]{3,2,1,0:T(4,128)S(1)}, f32[6,8,4,128]{3,2,1,0:T(4,128)S(1)}, f32[6,8,4,128,128]{4,3,2,1,0:T(8,128)}) %tuple.55, ...), branch_computations={%region_4.4_spmd, %region_5.7_spmd} | conditional | flops 1638973440 | bytes 73924640 | solution.py:66
  1054.0 19.8 collective-permute-done
  1090.7 23.2 %conditional.2 = ((f32[6,8,4,128]{3,2,1,0:T(4,128)S(1)}, f32[6,8,4,128]{3,2,1,0:T(4,128)S(1)}, f32[6,8,4,128,128]{4,3,2,1,0:T(8,128)})) conditional(s32[]{:T(128)} %convert_element_type.74, (f32[6,8,4,128]{3,2,1,0:T(4,128)S(1)}, f32[6,8,4,128]{3,2,1,0:T(4,128)S(1)}, f32[6,8,4,128,128]{4,3,2,1,0:T(8,128)}) %tuple.55, ...), branch_computations={%region_4.4_spmd, %region_5.7_spmd} | conditional | flops 1638973440 | bytes 73924640 | solution.py:66
  1116.3 19.8 collective-permute-done
  1153.0 23.2 %conditional.2 = ((f32[6,8,4,128]{3,2,1,0:T(4,128)S(1)}, f32[6,8,4,128]{3,2,1,0:T(4,128)S(1)}, f32[6,8,4,128,128]{4,3,2,1,0:T(8,128)})) conditional(s32[]{:T(128)} %convert_element_type.74, (f32[6,8,4,128]{3,2,1,0:T(4,128)S(1)}, f32[6,8,4,128]{3,2,1,0:T(4,128)S(1)}, f32[6,8,4,128,128]{4,3,2,1,0:T(8,128)}) %tuple.55, ...), branch_computations={%region_4.4_spmd, %region_5.7_spmd} | conditional | flops 1638973440 | bytes 73924640 | solution.py:66
  1178.6 19.8 collective-permute-done
  1215.3 23.2 %conditional.2 = ((f32[6,8,4,128]{3,2,1,0:T(4,128)S(1)}, f32[6,8,4,128]{3,2,1,0:T(4,128)S(1)}, f32[6,8,4,128,128]{4,3,2,1,0:T(8,128)})) conditional(s32[]{:T(128)} %convert_element_type.74, (f32[6,8,4,128]{3,2,1,0:T(4,128)S(1)}, f32[6,8,4,128]{3,2,1,0:T(4,128)S(1)}, f32[6,8,4,128,128]{4,3,2,1,0:T(8,128)}) %tuple.55, ...), branch_computations={%region_4.4_spmd, %region_5.7_spmd} | conditional | flops 1638973440 | bytes 73924640 | solution.py:66
  1240.9 19.8 collective-permute-done
  1277.6 23.2 %conditional.2 = ((f32[6,8,4,128]{3,2,1,0:T(4,128)S(1)}, f32[6,8,4,128]{3,2,1,0:T(4,128)S(1)}, f32[6,8,4,128,128]{4,3,2,1,0:T(8,128)})) conditional(s32[]{:T(128)} %convert_element_type.74, (f32[6,8,4,128]{3,2,1,0:T(4,128)S(1)}, f32[6,8,4,128]{3,2,1,0:T(4,128)S(1)}, f32[6,8,4,128,128]{4,3,2,1,0:T(8,128)}) %tuple.55, ...), branch_computations={%region_4.4_spmd, %region_5.7_spmd} | conditional | flops 1638973440 | bytes 73924640 | solution.py:66
  1303.2 19.8 collective-permute-done
  1339.9 23.2 %conditional.2 = ((f32[6,8,4,128]{3,2,1,0:T(4,128)S(1)}, f32[6,8,4,128]{3,2,1,0:T(4,128)S(1)}, f32[6,8,4,128,128]{4,3,2,1,0:T(8,128)})) conditional(s32[]{:T(128)} %convert_element_type.74, (f32[6,8,4,128]{3,2,1,0:T(4,128)S(1)}, f32[6,8,4,128]{3,2,1,0:T(4,128)S(1)}, f32[6,8,4,128,128]{4,3,2,1,0:T(8,128)}) %tuple.55, ...), branch_computations={%region_4.4_spmd, %region_5.7_spmd} | conditional | flops 1638973440 | bytes 73924640 | solution.py:66
  1365.5 19.8 collective-permute-done
  1402.2 23.2 %conditional.2 = ((f32[6,8,4,128]{3,2,1,0:T(4,128)S(1)}, f32[6,8,4,128]{3,2,1,0:T(4,128)S(1)}, f32[6,8,4,128,128]{4,3,2,1,0:T(8,128)})) conditional(s32[]{:T(128)} %convert_element_type.74, (f32[6,8,4,128]{3,2,1,0:T(4,128)S(1)}, f32[6,8,4,128]{3,2,1,0:T(4,128)S(1)}, f32[6,8,4,128,128]{4,3,2,1,0:T(8,128)}) %tuple.55, ...), branch_computations={%region_4.4_spmd, %region_5.7_spmd} | conditional | flops 1638973440 | bytes 73924640 | solution.py:66
  1427.8 19.8 collective-permute-done
  1464.5 23.2 %conditional.2 = ((f32[6,8,4,128]{3,2,1,0:T(4,128)S(1)}, f32[6,8,4,128]{3,2,1,0:T(4,128)S(1)}, f32[6,8,4,128,128]{4,3,2,1,0:T(8,128)})) conditional(s32[]{:T(128)} %convert_element_type.74, (f32[6,8,4,128]{3,2,1,0:T(4,128)S(1)}, f32[6,8,4,128]{3,2,1,0:T(4,128)S(1)}, f32[6,8,4,128,128]{4,3,2,1,0:T(8,128)}) %tuple.55, ...), branch_computations={%region_4.4_spmd, %region_5.7_spmd} | conditional | flops 1638973440 | bytes 73924640 | solution.py:66
  1490.1 19.8 collective-permute-done
  1526.8 23.2 %conditional.2 = ((f32[6,8,4,128]{3,2,1,0:T(4,128)S(1)}, f32[6,8,4,128]{3,2,1,0:T(4,128)S(1)}, f32[6,8,4,128,128]{4,3,2,1,0:T(8,128)})) conditional(s32[]{:T(128)} %convert_element_type.74, (f32[6,8,4,128]{3,2,1,0:T(4,128)S(1)}, f32[6,8,4,128]{3,2,1,0:T(4,128)S(1)}, f32[6,8,4,128,128]{4,3,2,1,0:T(8,128)}) %tuple.55, ...), branch_computations={%region_4.4_spmd, %region_5.7_spmd} | conditional | flops 1638973440 | bytes 73924640 | solution.py:66
  1552.4 19.8 collective-permute-done
  1589.1 23.2 %conditional.2 = ((f32[6,8,4,128]{3,2,1,0:T(4,128)S(1)}, f32[6,8,4,128]{3,2,1,0:T(4,128)S(1)}, f32[6,8,4,128,128]{4,3,2,1,0:T(8,128)})) conditional(s32[]{:T(128)} %convert_element_type.74, (f32[6,8,4,128]{3,2,1,0:T(4,128)S(1)}, f32[6,8,4,128]{3,2,1,0:T(4,128)S(1)}, f32[6,8,4,128,128]{4,3,2,1,0:T(8,128)}) %tuple.55, ...), branch_computations={%region_4.4_spmd, %region_5.7_spmd} | conditional | flops 1638973440 | bytes 73924640 | solution.py:66
  1614.7 19.8 collective-permute-done
  1651.4 23.2 %conditional.2 = ((f32[6,8,4,128]{3,2,1,0:T(4,128)S(1)}, f32[6,8,4,128]{3,2,1,0:T(4,128)S(1)}, f32[6,8,4,128,128]{4,3,2,1,0:T(8,128)})) conditional(s32[]{:T(128)} %convert_element_type.74, (f32[6,8,4,128]{3,2,1,0:T(4,128)S(1)}, f32[6,8,4,128]{3,2,1,0:T(4,128)S(1)}, f32[6,8,4,128,128]{4,3,2,1,0:T(8,128)}) %tuple.55, ...), branch_computations={%region_4.4_spmd, %region_5.7_spmd} | conditional | flops 1638973440 | bytes 73924640 | solution.py:66
  1677.0 19.8 collective-permute-done
  1713.7 23.2 %conditional.2 = ((f32[6,8,4,128]{3,2,1,0:T(4,128)S(1)}, f32[6,8,4,128]{3,2,1,0:T(4,128)S(1)}, f32[6,8,4,128,128]{4,3,2,1,0:T(8,128)})) conditional(s32[]{:T(128)} %convert_element_type.74, (f32[6,8,4,128]{3,2,1,0:T(4,128)S(1)}, f32[6,8,4,128]{3,2,1,0:T(4,128)S(1)}, f32[6,8,4,128,128]{4,3,2,1,0:T(8,128)}) %tuple.55, ...), branch_computations={%region_4.4_spmd, %region_5.7_spmd} | conditional | flops 1638973440 | bytes 73924640 | solution.py:66
  1739.3 19.8 collective-permute-done
  1776.0 23.2 %conditional.2 = ((f32[6,8,4,128]{3,2,1,0:T(4,128)S(1)}, f32[6,8,4,128]{3,2,1,0:T(4,128)S(1)}, f32[6,8,4,128,128]{4,3,2,1,0:T(8,128)})) conditional(s32[]{:T(128)} %convert_element_type.74, (f32[6,8,4,128]{3,2,1,0:T(4,128)S(1)}, f32[6,8,4,128]{3,2,1,0:T(4,128)S(1)}, f32[6,8,4,128,128]{4,3,2,1,0:T(8,128)}) %tuple.55, ...), branch_computations={%region_4.4_spmd, %region_5.7_spmd} | conditional | flops 1638973440 | bytes 73924640 | solution.py:66
  1801.6 19.8 collective-permute-done
  1838.3 23.2 %conditional.2 = ((f32[6,8,4,128]{3,2,1,0:T(4,128)S(1)}, f32[6,8,4,128]{3,2,1,0:T(4,128)S(1)}, f32[6,8,4,128,128]{4,3,2,1,0:T(8,128)})) conditional(s32[]{:T(128)} %convert_element_type.74, (f32[6,8,4,128]{3,2,1,0:T(4,128)S(1)}, f32[6,8,4,128]{3,2,1,0:T(4,128)S(1)}, f32[6,8,4,128,128]{4,3,2,1,0:T(8,128)}) %tuple.55, ...), branch_computations={%region_4.4_spmd, %region_5.7_spmd} | conditional | flops 1638973440 | bytes 73924640 | solution.py:66
  1863.9 19.8 collective-permute-done
  1900.6 23.2 %conditional.2 = ((f32[6,8,4,128]{3,2,1,0:T(4,128)S(1)}, f32[6,8,4,128]{3,2,1,0:T(4,128)S(1)}, f32[6,8,4,128,128]{4,3,2,1,0:T(8,128)})) conditional(s32[]{:T(128)} %convert_element_type.74, (f32[6,8,4,128]{3,2,1,0:T(4,128)S(1)}, f32[6,8,4,128]{3,2,1,0:T(4,128)S(1)}, f32[6,8,4,128,128]{4,3,2,1,0:T(8,128)}) %tuple.55, ...), branch_computations={%region_4.4_spmd, %region_5.7_spmd} | conditional | flops 1638973440 | bytes 73924640 | solution.py:66
  1926.2 19.8 collective-permute-done
  1962.8 23.2 %conditional.2 = ((f32[6,8,4,128]{3,2,1,0:T(4,128)S(1)}, f32[6,8,4,128]{3,2,1,0:T(4,128)S(1)}, f32[6,8,4,128,128]{4,3,2,1,0:T(8,128)})) conditional(s32[]{:T(128)} %convert_element_type.74, (f32[6,8,4,128]{3,2,1,0:T(4,128)S(1)}, f32[6,8,4,128]{3,2,1,0:T(4,128)S(1)}, f32[6,8,4,128,128]{4,3,2,1,0:T(8,128)}) %tuple.55, ...), branch_computations={%region_4.4_spmd, %region_5.7_spmd} | conditional | flops 1638973440 | bytes 73924640 | solution.py:66
  1988.5 19.8 collective-permute-done
  2027.6 38.7 %fusion.17 = bf16[6,128,4096]{2,1,0:T(8,128)(2,1)} fusion(bf16[6,128,4096]{2,1,0:T(8,128)(2,1)} %param.11, bf16[8,4,128,4096,1]{3,2,1,0,4:T(8,128)(2,1)} %bitcast.114, f32[6,8,4,128,128]{4,3,2,1,0:T(8,128)} %get-tuple-element.247, f32[6,8,4,128]{3,2,1,0:T(4,128)S(1)} %get-tuple-element.248), kind=kOutput, calls=%fused_computation.22 | convolution fusion | flops 25785532416 | bytes 58818560 | tf_op jit(solution)/shard_map/bkgqd,kgde->bqe/dot_general | solution.py:72
  (370 shorter events, 1378.9 us)
Async XLA Ops:
  17.6 5.0 slice-start
  88.2 4.5 copy-start
  119.5 19.9 collective-permute-start
  119.6 36.7 %collective-permute-start.1 = (bf16[6,128,8,128]{3,1,2,0:T(8,128)(2,1)}, bf16[6,128,8,128]{3,1,2,0:T(8,128)(2,1)S(1)}, u32[]{:S(2)}, u32[]{:S(2)}) collective-permute-start(bf16[6,128,8,128]{3,1,2,0:T(8,128)(2,1)} %get-tuple-element.366), channel_id=1, source_target_pairs={{0,1},{1,2},{2,3},{3,4},{4,5},{5,6},{6,7},{7,8},{8,9},{9,10},{10,1... | collective-permute-start | bytes 4718600 | tf_op jit(solution)/shard_map/while/body/eval_jaxpr/ppermute | solution.py:64
  181.9 19.8 collective-permute-start
  181.9 36.7 %collective-permute-start.1 = (bf16[6,128,8,128]{3,1,2,0:T(8,128)(2,1)}, bf16[6,128,8,128]{3,1,2,0:T(8,128)(2,1)S(1)}, u32[]{:S(2)}, u32[]{:S(2)}) collective-permute-start(bf16[6,128,8,128]{3,1,2,0:T(8,128)(2,1)} %get-tuple-element.366), channel_id=1, source_target_pairs={{0,1},{1,2},{2,3},{3,4},{4,5},{5,6},{6,7},{7,8},{8,9},{9,10},{10,1... | collective-permute-start | bytes 4718600 | tf_op jit(solution)/shard_map/while/body/eval_jaxpr/ppermute | solution.py:64
  244.2 19.8 collective-permute-start
  244.2 36.7 %collective-permute-start.1 = (bf16[6,128,8,128]{3,1,2,0:T(8,128)(2,1)}, bf16[6,128,8,128]{3,1,2,0:T(8,128)(2,1)S(1)}, u32[]{:S(2)}, u32[]{:S(2)}) collective-permute-start(bf16[6,128,8,128]{3,1,2,0:T(8,128)(2,1)} %get-tuple-element.366), channel_id=1, source_target_pairs={{0,1},{1,2},{2,3},{3,4},{4,5},{5,6},{6,7},{7,8},{8,9},{9,10},{10,1... | collective-permute-start | bytes 4718600 | tf_op jit(solution)/shard_map/while/body/eval_jaxpr/ppermute | solution.py:64
  306.5 19.8 collective-permute-start
  306.5 36.7 %collective-permute-start.1 = (bf16[6,128,8,128]{3,1,2,0:T(8,128)(2,1)}, bf16[6,128,8,128]{3,1,2,0:T(8,128)(2,1)S(1)}, u32[]{:S(2)}, u32[]{:S(2)}) collective-permute-start(bf16[6,128,8,128]{3,1,2,0:T(8,128)(2,1)} %get-tuple-element.366), channel_id=1, source_target_pairs={{0,1},{1,2},{2,3},{3,4},{4,5},{5,6},{6,7},{7,8},{8,9},{9,10},{10,1... | collective-permute-start | bytes 4718600 | tf_op jit(solution)/shard_map/while/body/eval_jaxpr/ppermute | solution.py:64
  368.8 19.8 collective-permute-start
  368.8 36.7 %collective-permute-start.1 = (bf16[6,128,8,128]{3,1,2,0:T(8,128)(2,1)}, bf16[6,128,8,128]{3,1,2,0:T(8,128)(2,1)S(1)}, u32[]{:S(2)}, u32[]{:S(2)}) collective-permute-start(bf16[6,128,8,128]{3,1,2,0:T(8,128)(2,1)} %get-tuple-element.366), channel_id=1, source_target_pairs={{0,1},{1,2},{2,3},{3,4},{4,5},{5,6},{6,7},{7,8},{8,9},{9,10},{10,1... | collective-permute-start | bytes 4718600 | tf_op jit(solution)/shard_map/while/body/eval_jaxpr/ppermute | solution.py:64
  431.1 19.8 collective-permute-start
  431.1 36.7 %collective-permute-start.1 = (bf16[6,128,8,128]{3,1,2,0:T(8,128)(2,1)}, bf16[6,128,8,128]{3,1,2,0:T(8,128)(2,1)S(1)}, u32[]{:S(2)}, u32[]{:S(2)}) collective-permute-start(bf16[6,128,8,128]{3,1,2,0:T(8,128)(2,1)} %get-tuple-element.366), channel_id=1, source_target_pairs={{0,1},{1,2},{2,3},{3,4},{4,5},{5,6},{6,7},{7,8},{8,9},{9,10},{10,1... | collective-permute-start | bytes 4718600 | tf_op jit(solution)/shard_map/while/body/eval_jaxpr/ppermute | solution.py:64
  493.4 19.8 collective-permute-start
  493.4 36.7 %collective-permute-start.1 = (bf16[6,128,8,128]{3,1,2,0:T(8,128)(2,1)}, bf16[6,128,8,128]{3,1,2,0:T(8,128)(2,1)S(1)}, u32[]{:S(2)}, u32[]{:S(2)}) collective-permute-start(bf16[6,128,8,128]{3,1,2,0:T(8,128)(2,1)} %get-tuple-element.366), channel_id=1, source_target_pairs={{0,1},{1,2},{2,3},{3,4},{4,5},{5,6},{6,7},{7,8},{8,9},{9,10},{10,1... | collective-permute-start | bytes 4718600 | tf_op jit(solution)/shard_map/while/body/eval_jaxpr/ppermute | solution.py:64
  555.7 19.8 collective-permute-start
  555.7 36.7 %collective-permute-start.1 = (bf16[6,128,8,128]{3,1,2,0:T(8,128)(2,1)}, bf16[6,128,8,128]{3,1,2,0:T(8,128)(2,1)S(1)}, u32[]{:S(2)}, u32[]{:S(2)}) collective-permute-start(bf16[6,128,8,128]{3,1,2,0:T(8,128)(2,1)} %get-tuple-element.366), channel_id=1, source_target_pairs={{0,1},{1,2},{2,3},{3,4},{4,5},{5,6},{6,7},{7,8},{8,9},{9,10},{10,1... | collective-permute-start | bytes 4718600 | tf_op jit(solution)/shard_map/while/body/eval_jaxpr/ppermute | solution.py:64
  618.0 19.8 collective-permute-start
  618.0 36.7 %collective-permute-start.1 = (bf16[6,128,8,128]{3,1,2,0:T(8,128)(2,1)}, bf16[6,128,8,128]{3,1,2,0:T(8,128)(2,1)S(1)}, u32[]{:S(2)}, u32[]{:S(2)}) collective-permute-start(bf16[6,128,8,128]{3,1,2,0:T(8,128)(2,1)} %get-tuple-element.366), channel_id=1, source_target_pairs={{0,1},{1,2},{2,3},{3,4},{4,5},{5,6},{6,7},{7,8},{8,9},{9,10},{10,1... | collective-permute-start | bytes 4718600 | tf_op jit(solution)/shard_map/while/body/eval_jaxpr/ppermute | solution.py:64
  680.3 19.8 collective-permute-start
  680.3 36.7 %collective-permute-start.1 = (bf16[6,128,8,128]{3,1,2,0:T(8,128)(2,1)}, bf16[6,128,8,128]{3,1,2,0:T(8,128)(2,1)S(1)}, u32[]{:S(2)}, u32[]{:S(2)}) collective-permute-start(bf16[6,128,8,128]{3,1,2,0:T(8,128)(2,1)} %get-tuple-element.366), channel_id=1, source_target_pairs={{0,1},{1,2},{2,3},{3,4},{4,5},{5,6},{6,7},{7,8},{8,9},{9,10},{10,1... | collective-permute-start | bytes 4718600 | tf_op jit(solution)/shard_map/while/body/eval_jaxpr/ppermute | solution.py:64
  742.6 19.8 collective-permute-start
  742.6 36.7 %collective-permute-start.1 = (bf16[6,128,8,128]{3,1,2,0:T(8,128)(2,1)}, bf16[6,128,8,128]{3,1,2,0:T(8,128)(2,1)S(1)}, u32[]{:S(2)}, u32[]{:S(2)}) collective-permute-start(bf16[6,128,8,128]{3,1,2,0:T(8,128)(2,1)} %get-tuple-element.366), channel_id=1, source_target_pairs={{0,1},{1,2},{2,3},{3,4},{4,5},{5,6},{6,7},{7,8},{8,9},{9,10},{10,1... | collective-permute-start | bytes 4718600 | tf_op jit(solution)/shard_map/while/body/eval_jaxpr/ppermute | solution.py:64
  804.8 19.8 collective-permute-start
  804.9 36.7 %collective-permute-start.1 = (bf16[6,128,8,128]{3,1,2,0:T(8,128)(2,1)}, bf16[6,128,8,128]{3,1,2,0:T(8,128)(2,1)S(1)}, u32[]{:S(2)}, u32[]{:S(2)}) collective-permute-start(bf16[6,128,8,128]{3,1,2,0:T(8,128)(2,1)} %get-tuple-element.366), channel_id=1, source_target_pairs={{0,1},{1,2},{2,3},{3,4},{4,5},{5,6},{6,7},{7,8},{8,9},{9,10},{10,1... | collective-permute-start | bytes 4718600 | tf_op jit(solution)/shard_map/while/body/eval_jaxpr/ppermute | solution.py:64
  867.1 19.8 collective-permute-start
  867.1 36.7 %collective-permute-start.1 = (bf16[6,128,8,128]{3,1,2,0:T(8,128)(2,1)}, bf16[6,128,8,128]{3,1,2,0:T(8,128)(2,1)S(1)}, u32[]{:S(2)}, u32[]{:S(2)}) collective-permute-start(bf16[6,128,8,128]{3,1,2,0:T(8,128)(2,1)} %get-tuple-element.366), channel_id=1, source_target_pairs={{0,1},{1,2},{2,3},{3,4},{4,5},{5,6},{6,7},{7,8},{8,9},{9,10},{10,1... | collective-permute-start | bytes 4718600 | tf_op jit(solution)/shard_map/while/body/eval_jaxpr/ppermute | solution.py:64
  929.4 19.8 collective-permute-start
  929.4 36.7 %collective-permute-start.1 = (bf16[6,128,8,128]{3,1,2,0:T(8,128)(2,1)}, bf16[6,128,8,128]{3,1,2,0:T(8,128)(2,1)S(1)}, u32[]{:S(2)}, u32[]{:S(2)}) collective-permute-start(bf16[6,128,8,128]{3,1,2,0:T(8,128)(2,1)} %get-tuple-element.366), channel_id=1, source_target_pairs={{0,1},{1,2},{2,3},{3,4},{4,5},{5,6},{6,7},{7,8},{8,9},{9,10},{10,1... | collective-permute-start | bytes 4718600 | tf_op jit(solution)/shard_map/while/body/eval_jaxpr/ppermute | solution.py:64
  991.7 19.8 collective-permute-start
  991.7 36.7 %collective-permute-start.1 = (bf16[6,128,8,128]{3,1,2,0:T(8,128)(2,1)}, bf16[6,128,8,128]{3,1,2,0:T(8,128)(2,1)S(1)}, u32[]{:S(2)}, u32[]{:S(2)}) collective-permute-start(bf16[6,128,8,128]{3,1,2,0:T(8,128)(2,1)} %get-tuple-element.366), channel_id=1, source_target_pairs={{0,1},{1,2},{2,3},{3,4},{4,5},{5,6},{6,7},{7,8},{8,9},{9,10},{10,1... | collective-permute-start | bytes 4718600 | tf_op jit(solution)/shard_map/while/body/eval_jaxpr/ppermute | solution.py:64
  1054.0 19.8 collective-permute-start
  1054.0 36.7 %collective-permute-start.1 = (bf16[6,128,8,128]{3,1,2,0:T(8,128)(2,1)}, bf16[6,128,8,128]{3,1,2,0:T(8,128)(2,1)S(1)}, u32[]{:S(2)}, u32[]{:S(2)}) collective-permute-start(bf16[6,128,8,128]{3,1,2,0:T(8,128)(2,1)} %get-tuple-element.366), channel_id=1, source_target_pairs={{0,1},{1,2},{2,3},{3,4},{4,5},{5,6},{6,7},{7,8},{8,9},{9,10},{10,1... | collective-permute-start | bytes 4718600 | tf_op jit(solution)/shard_map/while/body/eval_jaxpr/ppermute | solution.py:64
  1116.3 19.8 collective-permute-start
  1116.3 36.7 %collective-permute-start.1 = (bf16[6,128,8,128]{3,1,2,0:T(8,128)(2,1)}, bf16[6,128,8,128]{3,1,2,0:T(8,128)(2,1)S(1)}, u32[]{:S(2)}, u32[]{:S(2)}) collective-permute-start(bf16[6,128,8,128]{3,1,2,0:T(8,128)(2,1)} %get-tuple-element.366), channel_id=1, source_target_pairs={{0,1},{1,2},{2,3},{3,4},{4,5},{5,6},{6,7},{7,8},{8,9},{9,10},{10,1... | collective-permute-start | bytes 4718600 | tf_op jit(solution)/shard_map/while/body/eval_jaxpr/ppermute | solution.py:64
  1178.6 19.8 collective-permute-start
  1178.6 36.7 %collective-permute-start.1 = (bf16[6,128,8,128]{3,1,2,0:T(8,128)(2,1)}, bf16[6,128,8,128]{3,1,2,0:T(8,128)(2,1)S(1)}, u32[]{:S(2)}, u32[]{:S(2)}) collective-permute-start(bf16[6,128,8,128]{3,1,2,0:T(8,128)(2,1)} %get-tuple-element.366), channel_id=1, source_target_pairs={{0,1},{1,2},{2,3},{3,4},{4,5},{5,6},{6,7},{7,8},{8,9},{9,10},{10,1... | collective-permute-start | bytes 4718600 | tf_op jit(solution)/shard_map/while/body/eval_jaxpr/ppermute | solution.py:64
  1240.9 19.8 collective-permute-start
  1240.9 36.7 %collective-permute-start.1 = (bf16[6,128,8,128]{3,1,2,0:T(8,128)(2,1)}, bf16[6,128,8,128]{3,1,2,0:T(8,128)(2,1)S(1)}, u32[]{:S(2)}, u32[]{:S(2)}) collective-permute-start(bf16[6,128,8,128]{3,1,2,0:T(8,128)(2,1)} %get-tuple-element.366), channel_id=1, source_target_pairs={{0,1},{1,2},{2,3},{3,4},{4,5},{5,6},{6,7},{7,8},{8,9},{9,10},{10,1... | collective-permute-start | bytes 4718600 | tf_op jit(solution)/shard_map/while/body/eval_jaxpr/ppermute | solution.py:64
  1303.2 19.8 collective-permute-start
  1303.2 36.7 %collective-permute-start.1 = (bf16[6,128,8,128]{3,1,2,0:T(8,128)(2,1)}, bf16[6,128,8,128]{3,1,2,0:T(8,128)(2,1)S(1)}, u32[]{:S(2)}, u32[]{:S(2)}) collective-permute-start(bf16[6,128,8,128]{3,1,2,0:T(8,128)(2,1)} %get-tuple-element.366), channel_id=1, source_target_pairs={{0,1},{1,2},{2,3},{3,4},{4,5},{5,6},{6,7},{7,8},{8,9},{9,10},{10,1... | collective-permute-start | bytes 4718600 | tf_op jit(solution)/shard_map/while/body/eval_jaxpr/ppermute | solution.py:64
  1365.5 19.8 collective-permute-start
  1365.5 36.7 %collective-permute-start.1 = (bf16[6,128,8,128]{3,1,2,0:T(8,128)(2,1)}, bf16[6,128,8,128]{3,1,2,0:T(8,128)(2,1)S(1)}, u32[]{:S(2)}, u32[]{:S(2)}) collective-permute-start(bf16[6,128,8,128]{3,1,2,0:T(8,128)(2,1)} %get-tuple-element.366), channel_id=1, source_target_pairs={{0,1},{1,2},{2,3},{3,4},{4,5},{5,6},{6,7},{7,8},{8,9},{9,10},{10,1... | collective-permute-start | bytes 4718600 | tf_op jit(solution)/shard_map/while/body/eval_jaxpr/ppermute | solution.py:64
  1427.8 19.8 collective-permute-start
  1427.8 36.7 %collective-permute-start.1 = (bf16[6,128,8,128]{3,1,2,0:T(8,128)(2,1)}, bf16[6,128,8,128]{3,1,2,0:T(8,128)(2,1)S(1)}, u32[]{:S(2)}, u32[]{:S(2)}) collective-permute-start(bf16[6,128,8,128]{3,1,2,0:T(8,128)(2,1)} %get-tuple-element.366), channel_id=1, source_target_pairs={{0,1},{1,2},{2,3},{3,4},{4,5},{5,6},{6,7},{7,8},{8,9},{9,10},{10,1... | collective-permute-start | bytes 4718600 | tf_op jit(solution)/shard_map/while/body/eval_jaxpr/ppermute | solution.py:64
  1490.1 19.8 collective-permute-start
  1490.1 36.7 %collective-permute-start.1 = (bf16[6,128,8,128]{3,1,2,0:T(8,128)(2,1)}, bf16[6,128,8,128]{3,1,2,0:T(8,128)(2,1)S(1)}, u32[]{:S(2)}, u32[]{:S(2)}) collective-permute-start(bf16[6,128,8,128]{3,1,2,0:T(8,128)(2,1)} %get-tuple-element.366), channel_id=1, source_target_pairs={{0,1},{1,2},{2,3},{3,4},{4,5},{5,6},{6,7},{7,8},{8,9},{9,10},{10,1... | collective-permute-start | bytes 4718600 | tf_op jit(solution)/shard_map/while/body/eval_jaxpr/ppermute | solution.py:64
  1552.4 19.8 collective-permute-start
  1552.4 36.7 %collective-permute-start.1 = (bf16[6,128,8,128]{3,1,2,0:T(8,128)(2,1)}, bf16[6,128,8,128]{3,1,2,0:T(8,128)(2,1)S(1)}, u32[]{:S(2)}, u32[]{:S(2)}) collective-permute-start(bf16[6,128,8,128]{3,1,2,0:T(8,128)(2,1)} %get-tuple-element.366), channel_id=1, source_target_pairs={{0,1},{1,2},{2,3},{3,4},{4,5},{5,6},{6,7},{7,8},{8,9},{9,10},{10,1... | collective-permute-start | bytes 4718600 | tf_op jit(solution)/shard_map/while/body/eval_jaxpr/ppermute | solution.py:64
  1614.7 19.8 collective-permute-start
  1614.7 36.7 %collective-permute-start.1 = (bf16[6,128,8,128]{3,1,2,0:T(8,128)(2,1)}, bf16[6,128,8,128]{3,1,2,0:T(8,128)(2,1)S(1)}, u32[]{:S(2)}, u32[]{:S(2)}) collective-permute-start(bf16[6,128,8,128]{3,1,2,0:T(8,128)(2,1)} %get-tuple-element.366), channel_id=1, source_target_pairs={{0,1},{1,2},{2,3},{3,4},{4,5},{5,6},{6,7},{7,8},{8,9},{9,10},{10,1... | collective-permute-start | bytes 4718600 | tf_op jit(solution)/shard_map/while/body/eval_jaxpr/ppermute | solution.py:64
  1677.0 19.8 collective-permute-start
  1677.0 36.7 %collective-permute-start.1 = (bf16[6,128,8,128]{3,1,2,0:T(8,128)(2,1)}, bf16[6,128,8,128]{3,1,2,0:T(8,128)(2,1)S(1)}, u32[]{:S(2)}, u32[]{:S(2)}) collective-permute-start(bf16[6,128,8,128]{3,1,2,0:T(8,128)(2,1)} %get-tuple-element.366), channel_id=1, source_target_pairs={{0,1},{1,2},{2,3},{3,4},{4,5},{5,6},{6,7},{7,8},{8,9},{9,10},{10,1... | collective-permute-start | bytes 4718600 | tf_op jit(solution)/shard_map/while/body/eval_jaxpr/ppermute | solution.py:64
  1739.3 19.8 collective-permute-start
  1739.3 36.7 %collective-permute-start.1 = (bf16[6,128,8,128]{3,1,2,0:T(8,128)(2,1)}, bf16[6,128,8,128]{3,1,2,0:T(8,128)(2,1)S(1)}, u32[]{:S(2)}, u32[]{:S(2)}) collective-permute-start(bf16[6,128,8,128]{3,1,2,0:T(8,128)(2,1)} %get-tuple-element.366), channel_id=1, source_target_pairs={{0,1},{1,2},{2,3},{3,4},{4,5},{5,6},{6,7},{7,8},{8,9},{9,10},{10,1... | collective-permute-start | bytes 4718600 | tf_op jit(solution)/shard_map/while/body/eval_jaxpr/ppermute | solution.py:64
  1801.6 19.8 collective-permute-start
  1801.6 36.7 %collective-permute-start.1 = (bf16[6,128,8,128]{3,1,2,0:T(8,128)(2,1)}, bf16[6,128,8,128]{3,1,2,0:T(8,128)(2,1)S(1)}, u32[]{:S(2)}, u32[]{:S(2)}) collective-permute-start(bf16[6,128,8,128]{3,1,2,0:T(8,128)(2,1)} %get-tuple-element.366), channel_id=1, source_target_pairs={{0,1},{1,2},{2,3},{3,4},{4,5},{5,6},{6,7},{7,8},{8,9},{9,10},{10,1... | collective-permute-start | bytes 4718600 | tf_op jit(solution)/shard_map/while/body/eval_jaxpr/ppermute | solution.py:64
  1863.9 19.8 collective-permute-start
  1863.9 36.7 %collective-permute-start.1 = (bf16[6,128,8,128]{3,1,2,0:T(8,128)(2,1)}, bf16[6,128,8,128]{3,1,2,0:T(8,128)(2,1)S(1)}, u32[]{:S(2)}, u32[]{:S(2)}) collective-permute-start(bf16[6,128,8,128]{3,1,2,0:T(8,128)(2,1)} %get-tuple-element.366), channel_id=1, source_target_pairs={{0,1},{1,2},{2,3},{3,4},{4,5},{5,6},{6,7},{7,8},{8,9},{9,10},{10,1... | collective-permute-start | bytes 4718600 | tf_op jit(solution)/shard_map/while/body/eval_jaxpr/ppermute | solution.py:64
  1926.2 19.8 collective-permute-start
  1926.2 36.7 %collective-permute-start.1 = (bf16[6,128,8,128]{3,1,2,0:T(8,128)(2,1)}, bf16[6,128,8,128]{3,1,2,0:T(8,128)(2,1)S(1)}, u32[]{:S(2)}, u32[]{:S(2)}) collective-permute-start(bf16[6,128,8,128]{3,1,2,0:T(8,128)(2,1)} %get-tuple-element.366), channel_id=1, source_target_pairs={{0,1},{1,2},{2,3},{3,4},{4,5},{5,6},{6,7},{7,8},{8,9},{9,10},{10,1... | collective-permute-start | bytes 4718600 | tf_op jit(solution)/shard_map/while/body/eval_jaxpr/ppermute | solution.py:64
  1988.4 19.8 collective-permute-start
  1988.5 36.7 %collective-permute-start.1 = (bf16[6,128,8,128]{3,1,2,0:T(8,128)(2,1)}, bf16[6,128,8,128]{3,1,2,0:T(8,128)(2,1)S(1)}, u32[]{:S(2)}, u32[]{:S(2)}) collective-permute-start(bf16[6,128,8,128]{3,1,2,0:T(8,128)(2,1)} %get-tuple-element.366), channel_id=1, source_target_pairs={{0,1},{1,2},{2,3},{3,4},{4,5},{5,6},{6,7},{7,8},{8,9},{9,10},{10,1... | collective-permute-start | bytes 4718600 | tf_op jit(solution)/shard_map/while/body/eval_jaxpr/ppermute | solution.py:64
  (2 other events, 5.3 us)
where the time goes:
time: 2080 us; the launch traced here: 2070 us
  waiting for transfers between devices  1140 us (55%)
  matrix products  672 us (32%)
  other arithmetic  159 us (8%)
  local copies, waits for them, and re-layouts  95.7 us (5%)
    ppermute x62, waiting for transfers between devices, step_fn(): k_blk, v_blk = lax.ppermute((k_blk, v_blk), 'cp', shift_pairs)  1140 us
    dot_general x31, matrix products, attend_block(): jnp.einsum('bkgqs,bskd->bkgqd', prob_blk, v_blk, preferred_element_type=j...  436 us
    dot_general x31, matrix products, attend_block(): jnp.einsum('bqkgd,bskd->bkgqs', q_grp, k_blk, preferred_element_type=jnp....  143 us
    reduce_sum x31, other arithmetic, attend_block(): new_sum = run_sum * rescale + jnp.sum(prob_blk, axis=-1)  130 us
    while x62, local copies, waits for them, and re-layouts  74.7 us
  transfers between devices with their start and end apart: 62, of which 62 were waited for; matrix products, arithmetic and copies ran while one was open for 0% of the time, Pallas kernels for 0%

commit v1 on v0

v1 whole, which is shorter than its diff:
```python
import functools

import jax
import jax.numpy as jnp
from jax import lax
from jax.experimental import pallas as pl
from jax.experimental.pallas import tpu as pltpu
from jax.sharding import PartitionSpec as P

AXIS = 'cp'
LOG2E = 1.4426950408889634
VMEM_LIMIT = 60 * 1024 * 1024


def rms_norm(hidden, norm_gain):
    x_f32 = hidden.astype(jnp.float32)
    inv_rms = lax.rsqrt(jnp.mean(x_f32 * x_f32, axis=-1, keepdims=True) + 1e-5)
    return (x_f32 * inv_rms * norm_gain.astype(jnp.float32)).astype(jnp.bfloat16)


def rotary_tables(positions, head_dim):
    half_dim = head_dim // 2
    inv_freq = 10000.0 ** (-2.0 * jnp.arange(half_dim, dtype=jnp.float32) / head_dim)
    angles = positions.astype(jnp.float32)[:, :, None] * inv_freq
    cos_part, sin_part = jnp.cos(angles), jnp.sin(angles)
    cos_tab = jnp.concatenate([cos_part, cos_part], axis=-1)
    sin_tab = jnp.concatenate([-sin_part, sin_part], axis=-1)
    return cos_tab.reshape(-1, head_dim), sin_tab.reshape(-1, head_dim)


def group_barrier(me, n_cp):
    barrier = pltpu.get_barrier_semaphore()

    def signal(k, _):
        pl.semaphore_signal(barrier, inc=1, device_id={AXIS: lax.rem(me + k, n_cp)}, device_id_type=pl.DeviceIdType.MESH)
        return 0

    lax.fori_loop(1, n_cp, signal, 0)
    pl.semaphore_wait(barrier, n_cp - 1)


def put(src, dst, owner, me, send_sem, recv_sem):
    @pl.when(owner == me)
    def _():
        pltpu.make_async_copy(src, dst, recv_sem).start()

    @pl.when(owner != me)
    def _():
        pltpu.make_async_remote_copy(src, dst, send_sem, recv_sem, device_id={AXIS: owner}, device_id_type=pl.DeviceIdType.MESH).start()


def wait_bytes_of(ref, sem):
    pltpu.make_async_copy(ref, ref, sem).wait()


def project_kernel(n_cp, n_kv, per_dev, h_ref, cos_ref, sin_ref, wq_ref, wk_ref, wv_ref, q_out, kv_out, w_buf, acc, stage, w_sem, send_sem, recv_q, recv_kv):
    me = lax.axis_index(AXIS)
    chip = me // 2
    n_steps, batch, seq, width = stage.shape
    head_dim = width // 2
    half_dim = head_dim // 2
    n_q = n_steps - n_kv

    def kv_block(step):
        return lax.rem(step + chip, n_kv)

    def q_block(step):
        return lax.rem(step - n_kv + chip, n_q)

    def fetch(step, slot):
        @pl.when(step < n_kv)
        def _():
            cols = pl.ds(pl.multiple_of(kv_block(step) * head_dim, head_dim), head_dim)
            pltpu.make_async_copy(wk_ref.at[:, cols], w_buf.at[slot, :, pl.ds(0, head_dim)], w_sem.at[slot]).start()
            pltpu.make_async_copy(wv_ref.at[:, cols], w_buf.at[slot, :, pl.ds(head_dim, head_dim)], w_sem.at[slot]).start()

        @pl.when(step >= n_kv)
        def _():
            cols = pl.ds(pl.multiple_of(q_block(step) * width, width), width)
            pltpu.make_async_copy(wq_ref.at[:, cols], w_buf.at[slot], w_sem.at[slot]).start()

    def send(step):
        @pl.when(step < n_kv)
        def _():
            head = kv_block(step)
            for b in range(batch):
                pair = b * n_kv + head
                first, second = (2 * pair) // per_dev, (2 * pair + 1) // per_dev
                src = stage.at[step, b]
                rows = pl.ds(me * seq, seq)
                put(src, kv_out.at[pair - (per_dev * first) // 2, rows], first, me, send_sem, recv_kv)

                @pl.when(second != first)
                def _():
                    put(src, kv_out.at[pair - (per_dev * second) // 2, rows], second, me, send_sem, recv_kv)

        @pl.when(step >= n_kv)
        def _():
            head = q_block(step)
            for b in range(batch):
                unit = b * n_q + head
                owner = unit // per_dev
                put(stage.at[step, b], q_out.at[unit - per_dev * owner, pl.ds(me * seq, seq)], owner, me, send_sem, recv_q)

    fetch(0, 0)
    group_barrier(me, n_cp)

    def rotate(x):
        return (x * cos_ref[...] + pltpu.roll(x, half_dim, 1) * sin_ref[...]).astype(jnp.bfloat16).reshape(batch, seq, head_dim)

    def body(step, _):
        slot = lax.rem(step, 2)
        wait_bytes_of(w_buf.at[slot], w_sem.at[slot])

        @pl.when(step + 1 < n_steps)
        def _():
            fetch(step + 1, 1 - slot)

        acc[...] = jnp.dot(h_ref[...], w_buf[slot], preferred_element_type=jnp.float32)
        stage[step, :, :, 0:head_dim] = rotate(acc[:, 0:head_dim])

        @pl.when(step < n_kv)
        def _():
            stage[step, :, :, head_dim:width] = acc[:, head_dim:width].astype(jnp.bfloat16).reshape(batch, seq, head_dim)

        @pl.when(step >= n_kv)
        def _():
            stage[step, :, :, head_dim:width] = rotate(acc[:, head_dim:width])

        @pl.when(step > 0)
        def _():
            send(step - 1)

        return 0

    lax.fori_loop(0, n_steps, body, 0)
    send(n_steps - 1)
    away = (n_cp - 1) * seq
    wait_bytes_of(q_out.at[:, pl.ds(0, away)], send_sem)
    wait_bytes_of(kv_out.at[:, pl.ds(0, away)], send_sem)
    wait_bytes_of(q_out, recv_q)
    wait_bytes_of(kv_out, recv_kv)


def attend_kernel(n_cp, per_dev, blk_q, blk_k, q_ref, kv_ref, o_out, v_t, stage, acc, send_sem, recv_sem):
    me = lax.axis_index(AXIS)
    n_units, total, width = q_ref.shape
    head_dim = width // 2
    batch, seq, model = o_out.shape
    n_q = model // width
    n_blocks = total // blk_q
    span = blk_q // seq
    factor = LOG2E * head_dim ** -0.5

    group_barrier(me, n_cp)
    for s in range(kv_ref.shape[0]):
        def turn(c, _):
            rows = pl.ds(pl.multiple_of(c * blk_k, blk_k), blk_k)
            v_t[s, :, rows] = kv_ref[s, rows, head_dim:width].astype(jnp.float32).T.astype(jnp.bfloat16)
            return 0

        lax.fori_loop(0, total // blk_k, turn, 0)

    def block_of(t):
        return lax.rem(t + me // 2 + 1, n_blocks)

    def send(t):
        unit, i = t // n_blocks, block_of(lax.rem(t, n_blocks))
        half = per_dev * me + unit
        b = half // n_q
        cols = pl.ds(pl.multiple_of(lax.rem(half, n_q) * width, width), width)
        for r in range(span):
            owner = i * span + r
            put(stage.at[unit, pl.ds(owner * seq, seq)], o_out.at[b, :, cols], owner, me, send_sem, recv_sem)

    def scores(kv_slot, start, size, q_head):
        k_blk = kv_ref[kv_slot, pl.ds(pl.multiple_of(start, blk_q), size), 0:head_dim]
        return lax.dot_general(k_blk, q_head, (((1,), (1,)), ((), ())), preferred_element_type=jnp.float32)

    def weigh(kv_slot, start, size, prob):
        return jnp.dot(v_t[kv_slot, :, pl.ds(pl.multiple_of(start, blk_q), size)], prob.astype(jnp.bfloat16), preferred_element_type=jnp.float32)

    def step(t, _):
        unit, i = t // n_blocks, block_of(lax.rem(t, n_blocks))
        kv_slot = (per_dev * me + unit) // 2 - (per_dev * me) // 2
        q_start = pl.multiple_of(i * blk_q, blk_q)
        q_rows = pl.ds(q_start, blk_q)
        q_heads = [q_ref[unit, q_rows, g * head_dim:(g + 1) * head_dim] for g in range(2)]

        def diagonal(size):
            start = q_start + blk_q - size
            allowed = lax.broadcasted_iota(jnp.int32, (size, blk_q), 0) - (size - blk_q) <= lax.broadcasted_iota(jnp.int32, (size, blk_q), 1)
            out = []
            for g in range(2):
                s = jnp.where(allowed, scores(kv_slot, start, size, q_heads[g]), -jnp.inf)
                top = jnp.max(s, axis=0, keepdims=True)
                prob = jnp.exp2(s * factor - top * factor)
                acc[g] = weigh(kv_slot, start, size, prob)
                out += [top, jnp.sum(prob, axis=0, keepdims=True)]
            return tuple(out)

        state = lax.cond(lax.rem(i, 2) == 0, lambda: diagonal(blk_q), lambda: diagonal(2 * blk_q))

        def full(j, state):
            start = j * blk_k
            all_s = [scores(kv_slot, start, blk_k, q_heads[g]) for g in range(2)]
            out = []
            for g in range(2):
                top, total_p = state[2 * g], state[2 * g + 1]
                s = all_s[g]
                new_top = jnp.maximum(top, jnp.max(s, axis=0, keepdims=True))
                prob = jnp.exp2(s * factor - new_top * factor)
                rescale = jnp.exp2(top * factor - new_top * factor)
                acc[g] = acc[g] * rescale + weigh(kv_slot, start, blk_k, prob)
                out += [new_top, total_p * rescale + jnp.sum(prob, axis=0, keepdims=True)]
            return tuple(out)

        state = lax.fori_loop(0, i // 2, full, state)
        for g in range(2):
            stage[unit, q_rows, g * head_dim:(g + 1) * head_dim] = (acc[g] / state[2 * g + 1]).T.astype(jnp.bfloat16)

        @pl.when(t > 0)
        def _():
            send(t - 1)

        return 0

    n_all = n_units * n_blocks
    lax.fori_loop(0, n_all, step, 0)
    send(n_all - 1)
    wait_bytes_of(stage.at[:, pl.ds(0, total - seq)], send_sem)
    wait_bytes_of(o_out, recv_sem)


def solution(mesh):
    n_cp = mesh.shape[AXIS]

    def local_block(hidden, positions, norm_gain, w_query, w_key, w_value, w_out):
        batch, seq, model_dim = hidden.shape
        n_heads, head_dim, _ = w_out.shape
        n_kv = w_key.shape[1] // head_dim
        width = 2 * head_dim
        n_q = n_heads // 2
        per_dev = batch * n_q // n_cp
        n_slots = per_dev // 2 + 1
        total = n_cp * seq
        n_steps = n_kv + n_q
        any_space = pl.BlockSpec(memory_space=pl.ANY)
        vmem = pl.BlockSpec(memory_space=pltpu.VMEM)
        normed = rms_norm(hidden, norm_gain).reshape(batch * seq, model_dim)
        cos_tab, sin_tab = rotary_tables(positions, head_dim)
        q_all, kv_all = pl.pallas_call(
            functools.partial(project_kernel, n_cp, n_kv, per_dev),
            out_shape=(
                jax.ShapeDtypeStruct((per_dev, total, width), jnp.bfloat16),
                jax.ShapeDtypeStruct((n_slots, total, width), jnp.bfloat16),
            ),
            in_specs=[vmem, vmem, vmem, any_space, any_space, any_space],
            out_specs=(any_space, any_space),
            scratch_shapes=[
                pltpu.VMEM((2, model_dim, width), jnp.bfloat16),
                pltpu.VMEM((batch * seq, width), jnp.float32),
                pltpu.VMEM((n_steps, batch, seq, width), jnp.bfloat16),
                pltpu.SemaphoreType.DMA((2,)),
                pltpu.SemaphoreType.DMA,
                pltpu.SemaphoreType.DMA,
                pltpu.SemaphoreType.DMA,
            ],
            compiler_params=pltpu.CompilerParams(collective_id=0, has_side_effects=True, vmem_limit_bytes=VMEM_LIMIT),
            name='project_and_send',
        )(normed, cos_tab, sin_tab, w_query, w_key, w_value)
        blk_q = 2 * seq
        attn_out = pl.pallas_call(
            functools.partial(attend_kernel, n_cp, per_dev, blk_q, 2 * blk_q),
            out_shape=jax.ShapeDtypeStruct((batch, seq, n_heads * head_dim), jnp.bfloat16),
            in_specs=[vmem, vmem],
            out_specs=any_space,
            scratch_shapes=[
                pltpu.VMEM((n_slots, head_dim, total), jnp.bfloat16),
                pltpu.VMEM((per_dev, total, width), jnp.bfloat16),
                pltpu.VMEM((2, head_dim, blk_q), jnp.float32),
                pltpu.SemaphoreType.DMA,
                pltpu.SemaphoreType.DMA,
            ],
            compiler_params=pltpu.CompilerParams(collective_id=1, has_side_effects=True, vmem_limit_bytes=VMEM_LIMIT),
            name='attend_and_return',
        )(q_all, kv_all)
        proj_out = jnp.einsum('bqe,ed->bqd', attn_out, w_out.reshape(n_heads * head_dim, model_dim), preferred_element_type=jnp.float32)
        return (hidden.astype(jnp.float32) + proj_out).astype(jnp.bfloat16)

    act_spec = P('dp', 'cp', None)
    return jax.shard_map(local_block, mesh=mesh, in_specs=(act_spec, P('dp', 'cp'), P(), P(), P(), P(), P()), out_specs=act_spec, check_vma=False)
```

time: 2080 us -> 391 us (0.19)
  the two profiles are of different devices: /device:TPU:126 before, /device:TPU:97 now
where the time goes in v1:
time: 391 us
  Pallas kernels  343 us (88%)
  matrix products  33.5 us (9%)
  other arithmetic  13.8 us (4%)
    pallas_call x1, Pallas kernels, local_block(): pl.pallas_call(functools.partial(attend_kernel, n_cp, per_dev, blk_q, 2 *...  197 us
    pallas_call x1, Pallas kernels, local_block(): pl.pallas_call(functools.partial(project_kernel, n_cp, n_kv, per_dev), ou...  146 us
    dot_general x1, matrix products, local_block(): jnp.einsum('bqe,ed->bqd', attn_out, w_out.reshape(n_heads * head_dim, mod...  33.5 us

profile of v1, /device:TPU:97, one launch (start us, length us, event | category | flops | bytes accessed | tf_op | source)
XLA Modules:
  0.0 390.8 jit_solution(17597492727478734512)
XLA Ops:
  0.0 0.0 copy-start
  0.0 0.8 convert_bitcast_fusion
  0.9 4.2 %fusion = f32[6,128]{1,0:T(8,128)S(1)} fusion(bf16[6,128,4096]{2,1,0:T(8,128)(2,1)} %param.7), kind=kLoop, calls=%fused_computation.3 | loop fusion | flops 9436416 | bytes 6294528 | tf_op jit(solution)/shard_map/reduce_sum | solution.py:17
  5.1 0.7 convert_element_type.17
  5.8 1.4 fusion.4
  7.2 1.2 pad_maximum_fusion
  8.4 0.0 copy-done
  8.4 5.4 %fusion.2 = bf16[6,128,4096]{2,1,0:T(8,128)(2,1)} fusion(bf16[6,128,4096]{2,1,0:T(8,128)(2,1)S(1)} %copy-done, f32[4096]{0:T(1024)S(1)} %convert_element_type.17, f32[6,128]{1,0:T(8,128)S(1)} %add_rsqrt_fusion), kind=kLoop, calls=%fused_computation.5 | loop fusion | flops 12582912 | bytes 12602368 | tf_op jit(solution)/shard_map/convert_element_type | solution.py:18
  13.8 146.3 %project_and_send.1 = (bf16[3,4096,256]{2,1,0:T(8,128)(2,1)}, bf16[2,4096,256]{2,1,0:T(8,128)(2,1)}) custom-call(bf16[768,4096]{1,0:T(8,128)(2,1)} %bitcast.8, f32[768,128]{1,0:T(8,128)} %get-tuple-element.12.cos_ref, f32[768,128]{1,0:T(8,128)} %get-tuple-element.13.sin_ref, bf16[4096,4096]{1,0:T(8,128)(2,1)} %wq_ref.1, bf16[4096,1024]{1,0:T(8,128)(2,1)} %wk_ref.1, ...), custom_call_target="tpu_custom_call" | custom-call | tf_op jit(solution)/shard_map/project_and_send/pallas_call | solution.py:252
  160.1 197.2 %attend_and_return.1 = bf16[6,128,4096]{2,1,0:T(8,128)(2,1)} custom-call(bf16[3,4096,256]{2,1,0:T(8,128)(2,1)} %get-tuple-element.7.q_ref, bf16[2,4096,256]{2,1,0:T(8,128)(2,1)} %get-tuple-element.8.kv_ref), custom_call_target="tpu_custom_call" | custom-call | tf_op jit(solution)/shard_map/attend_and_return/pallas_call | solution.py:273
  357.3 33.5 %fusion.3 = bf16[6,128,4096]{2,1,0:T(8,128)(2,1)} fusion(bf16[6,128,4096]{2,1,0:T(8,128)(2,1)} %param.7, bf16[6,128,4096]{2,1,0:T(8,128)(2,1)} %attend_and_return.1, bf16[4096,4096,1]{1,0,2:T(8,128)(2,1)} %bitcast.9), kind=kOutput, calls=%fused_computation.6 | convolution fusion | flops 25779240960 | bytes 52428800 | tf_op jit(solution)/shard_map/bqe,ed->bqd/dot_general | solution.py:288
  (2 shorter events, 0.0 us)
Async XLA Ops:
  0.0 8.4 %copy-start = (bf16[6,128,4096]{2,1,0:T(8,128)(2,1)S(1)}, bf16[6,128,4096]{2,1,0:T(8,128)(2,1)}, u32[]{:S(2)}) copy-start(bf16[6,128,4096]{2,1,0:T(8,128)(2,1)} %param.7) | copy-start | bytes 18874372

commit v2 on v1

--- a/solution.py
+++ b/solution.py
@@ -9,6 +9,7 @@
 
 AXIS = 'cp'
 LOG2E = 1.4426950408889634
+CHUNK = 32
 VMEM_LIMIT = 60 * 1024 * 1024
 
 
@@ -142,13 +143,15 @@
     wait_bytes_of(kv_out, recv_kv)
 
 
-def attend_kernel(n_cp, per_dev, blk_q, blk_k, q_ref, kv_ref, o_out, v_t, stage, acc, send_sem, recv_sem):
+def attend_kernel(n_cp, per_dev, blk_q, blk_k, q_ref, kv_ref, o_out, v_t, stage, s_buf, p_buf, acc, stat, send_sem, recv_sem):
     me = lax.axis_index(AXIS)
     n_units, total, width = q_ref.shape
     head_dim = width // 2
     batch, seq, model = o_out.shape
     n_q = model // width
     n_blocks = total // blk_q
+    n_all = n_units * n_blocks
+    ratio = blk_k // blk_q
     span = blk_q // seq
     factor = LOG2E * head_dim ** -0.5
 
@@ -161,11 +164,14 @@
 
         lax.fori_loop(0, total // blk_k, turn, 0)
 
-    def block_of(t):
-        return lax.rem(t + me // 2 + 1, n_blocks)
+    def place(t):
+        unit = t // n_blocks
+        i = lax.rem(lax.rem(t, n_blocks) + me // 2 + 1, n_blocks)
+        slot = (per_dev * me + unit) // 2 - (per_dev * me) // 2
+        return unit, slot, i, i // ratio
 
     def send(t):
-        unit, i = t // n_blocks, block_of(lax.rem(t, n_blocks))
+        unit, _, i, _ = place(t)
         half = per_dev * me + unit
         b = half // n_q
         cols = pl.ds(pl.multiple_of(lax.rem(half, n_q) * width, width), width)
@@ -173,60 +179,87 @@
             owner = i * span + r
             put(stage.at[unit, pl.ds(owner * seq, seq)], o_out.at[b, :, cols], owner, me, send_sem, recv_sem)
 
-    def scores(kv_slot, start, size, q_head):
-        k_blk = kv_ref[kv_slot, pl.ds(pl.multiple_of(start, blk_q), size), 0:head_dim]
-        return lax.dot_general(k_blk, q_head, (((1,), (1,)), ((), ())), preferred_element_type=jnp.float32)
-
-    def weigh(kv_slot, start, size, prob):
-        return jnp.dot(v_t[kv_slot, :, pl.ds(pl.multiple_of(start, blk_q), size)], prob.astype(jnp.bfloat16), preferred_element_type=jnp.float32)
+    def next_scores(unit, slot, i, j):
+        k_blk = kv_ref[slot, pl.ds(pl.multiple_of(j * blk_k, blk_k), blk_k), 0:head_dim]
+        q_rows = pl.ds(pl.multiple_of(i * blk_q, blk_q), blk_q)
+        for g in range(2):
+            q_head = q_ref[unit, q_rows, g * head_dim:(g + 1) * head_dim]
+            cols = slice(g * blk_q, (g + 1) * blk_q)
+            s = lax.dot_general(k_blk, q_head, (((1,), (1,)), ((), ())), preferred_element_type=jnp.float32)
+            s_buf[:, cols] = s
+            stat[3, 0:1, cols] = jnp.max(s, axis=0, keepdims=True)
+
+    def weighed(slot, j):
+        cols = pl.ds(pl.multiple_of(j * blk_k, blk_k), blk_k)
+        return acc[...] * stat[2, 0:1, :] + jnp.dot(v_t[slot, :, cols], p_buf[...], preferred_element_type=jnp.float32)
+
+    def finish(t):
+        unit, slot, i, n_full = place(t)
+        out = weighed(slot, jnp.maximum(n_full - 1, 0)) * (1.0 / stat[1, 0:1, :])
+        q_rows = pl.ds(pl.multiple_of(i * blk_q, blk_q), blk_q)
+        for g in range(2):
+            stage[unit, q_rows, g * head_dim:(g + 1) * head_dim] = out[:, g * blk_q:(g + 1) * blk_q].T.astype(jnp.bfloat16)
 
     def step(t, _):
-        unit, i = t // n_blocks, block_of(lax.rem(t, n_blocks))
-        kv_slot = (per_dev * me + unit) // 2 - (per_dev * me) // 2
-        q_start = pl.multiple_of(i * blk_q, blk_q)
-        q_rows = pl.ds(q_start, blk_q)
-        q_heads = [q_ref[unit, q_rows, g * head_dim:(g + 1) * head_dim] for g in range(2)]
+        unit, slot, i, n_full = place(t)
+        after = place(jnp.minimum(t + 1, n_all - 1))
+
+        def follow(j, n_done):
+            more = n_done < n_full
+            pick = lambda here, there: jnp.where(more, here, there)
+            next_scores(pick(unit, after[0]), pick(slot, after[1]), pick(i, after[2]), pick(n_done, after[3]))
+
+        @pl.when(t > 1)
+        def _():
+            send(t - 2)
 
         def diagonal(size):
-            start = q_start + blk_q - size
-            allowed = lax.broadcasted_iota(jnp.int32, (size, blk_q), 0) - (size - blk_q) <= lax.broadcasted_iota(jnp.int32, (size, blk_q), 1)
-            out = []
-            for g in range(2):
-                s = jnp.where(allowed, scores(kv_slot, start, size, q_heads[g]), -jnp.inf)
-                top = jnp.max(s, axis=0, keepdims=True)
-                prob = jnp.exp2(s * factor - top * factor)
-                acc[g] = weigh(kv_slot, start, size, prob)
-                out += [top, jnp.sum(prob, axis=0, keepdims=True)]
-            return tuple(out)
-
-        state = lax.cond(lax.rem(i, 2) == 0, lambda: diagonal(blk_q), lambda: diagonal(2 * blk_q))
-
-        def full(j, state):
-            start = j * blk_k
-            all_s = [scores(kv_slot, start, blk_k, q_heads[g]) for g in range(2)]
-            out = []
-            for g in range(2):
-                top, total_p = state[2 * g], state[2 * g + 1]
-                s = all_s[g]
-                new_top = jnp.maximum(top, jnp.max(s, axis=0, keepdims=True))
-                prob = jnp.exp2(s * factor - new_top * factor)
-                rescale = jnp.exp2(top * factor - new_top * factor)
-                acc[g] = acc[g] * rescale + weigh(kv_slot, start, blk_k, prob)
-                out += [new_top, total_p * rescale + jnp.sum(prob, axis=0, keepdims=True)]
-            return tuple(out)
-
-        state = lax.fori_loop(0, i // 2, full, state)
-        for g in range(2):
-            stage[unit, q_rows, g * head_dim:(g + 1) * head_dim] = (acc[g] / state[2 * g + 1]).T.astype(jnp.bfloat16)
-
-        @pl.when(t > 0)
-        def _():
-            send(t - 1)
-
+            finish(jnp.maximum(t - 1, 0))
+            acc[...] = jnp.zeros_like(acc)
+            shape = (size, 2 * blk_q)
+            allowed = lax.broadcasted_iota(jnp.int32, shape, 0) - (size - blk_q) <= lax.rem(lax.broadcasted_iota(jnp.int32, shape, 1), blk_q)
+            s = jnp.where(allowed, s_buf[0:size, :], -jnp.inf)
+            top = jnp.max(s, axis=0, keepdims=True)
+            prob = jnp.exp2(s * factor - top * factor)
+            stat[0, 0:1, :] = top
+            stat[1, 0:1, :] = jnp.sum(prob, axis=0, keepdims=True)
+            stat[2, 0:1, :] = jnp.ones_like(top)
+            p_buf[0:size, :] = prob.astype(jnp.bfloat16)
+            if size < blk_k:
+                p_buf[size:blk_k, :] = jnp.zeros((blk_k - size, 2 * blk_q), jnp.bfloat16)
+            follow(None, 0)
+
+        for r in range(ratio):
+            pl.when(lax.rem(i, ratio) == r)(functools.partial(diagonal, (r + 1) * blk_q))
+
+        def full(j, _):
+            acc[...] = weighed(slot, jnp.where(j == 0, n_full, j - 1))
+            top = stat[0, 0:1, :]
+            new_top = jnp.maximum(top, stat[3, 0:1, :])
+            shift = new_top * factor
+            rescale = jnp.exp2(top * factor - shift)
+            part = jnp.zeros((8, 2 * blk_q), jnp.float32)
+            for r in range(0, blk_k, CHUNK):
+                prob = jnp.exp2(s_buf[r:r + CHUNK, :] * factor - shift)
+                part = part + jnp.sum(prob.reshape(CHUNK // 8, 8, 2 * blk_q), axis=0)
+                p_buf[r:r + CHUNK, :] = prob.astype(jnp.bfloat16)
+            stat[0, 0:1, :] = new_top
+            stat[1, 0:1, :] = stat[1, 0:1, :] * rescale + jnp.sum(part, axis=0, keepdims=True)
+            stat[2, 0:1, :] = rescale
+            follow(j, j + 1)
+            return 0
+
+        lax.fori_loop(0, n_full, full, 0)
         return 0
 
-    n_all = n_units * n_blocks
+    acc[...] = jnp.zeros_like(acc)
+    stat[...] = jnp.ones_like(stat)
+    p_buf[...] = jnp.zeros_like(p_buf)
+    first = place(0)
+    next_scores(first[0], first[1], first[2], first[3])
     lax.fori_loop(0, n_all, step, 0)
+    send(n_all - 2)
+    finish(n_all - 1)
     send(n_all - 1)
     wait_bytes_of(stage.at[:, pl.ds(0, total - seq)], send_sem)
     wait_bytes_of(o_out, recv_sem)
@@ -278,7 +311,10 @@
             scratch_shapes=[
                 pltpu.VMEM((n_slots, head_dim, total), jnp.bfloat16),
                 pltpu.VMEM((per_dev, total, width), jnp.bfloat16),
-                pltpu.VMEM((2, head_dim, blk_q), jnp.float32),
+                pltpu.VMEM((2 * blk_q, 2 * blk_q), jnp.float32),
+                pltpu.VMEM((2 * blk_q, 2 * blk_q), jnp.bfloat16),
+                pltpu.VMEM((head_dim, 2 * blk_q), jnp.float32),
+                pltpu.VMEM((4, 8, 2 * blk_q), jnp.float32),
                 pltpu.SemaphoreType.DMA,
                 pltpu.SemaphoreType.DMA,
             ],

time: 391 us -> 313 us (0.80)
  Pallas kernels: 343 us -> 266 us
    pallas_call x1, Pallas kernels: 197 us -> 120 us  [local_block(): pl.pallas_call(functools.partial(attend_kernel, n_cp, per_dev, blk_q, 2 *...]
where the time goes in v2:
time: 313 us
  Pallas kernels  266 us (85%)
  matrix products  33.5 us (11%)
  other arithmetic  13.8 us (4%)
    pallas_call x1, Pallas kernels, local_block(): pl.pallas_call(functools.partial(project_kernel, n_cp, n_kv, per_dev), ou...  146 us
    pallas_call x1, Pallas kernels, local_block(): pl.pallas_call(functools.partial(attend_kernel, n_cp, per_dev, blk_q, 2 *...  120 us
    dot_general x1, matrix products, local_block(): jnp.einsum('bqe,ed->bqd', attn_out, w_out.reshape(n_heads * head_dim, mod...  33.5 us

profile of v2, /device:TPU:97, one launch (start us, length us, event | category | flops | bytes accessed | tf_op | source)
XLA Modules:
  0.0 313.2 jit_solution(2299588230844444354)
XLA Ops:
  0.0 0.0 copy-start
  0.0 0.8 convert_bitcast_fusion
  0.9 4.2 %fusion = f32[6,128]{1,0:T(8,128)S(1)} fusion(bf16[6,128,4096]{2,1,0:T(8,128)(2,1)} %param.7), kind=kLoop, calls=%fused_computation.3 | loop fusion | flops 9436416 | bytes 6294528 | tf_op jit(solution)/shard_map/reduce_sum | solution.py:18
  5.1 0.7 convert_element_type.17
  5.8 1.4 fusion.4
  7.2 1.2 pad_maximum_fusion
  8.4 0.0 copy-done
  8.4 5.4 %fusion.2 = bf16[6,128,4096]{2,1,0:T(8,128)(2,1)} fusion(bf16[6,128,4096]{2,1,0:T(8,128)(2,1)S(1)} %copy-done, f32[4096]{0:T(1024)S(1)} %convert_element_type.17, f32[6,128]{1,0:T(8,128)S(1)} %add_rsqrt_fusion), kind=kLoop, calls=%fused_computation.5 | loop fusion | flops 12582912 | bytes 12602368 | tf_op jit(solution)/shard_map/convert_element_type | solution.py:19
  13.8 146.3 %project_and_send.1 = (bf16[3,4096,256]{2,1,0:T(8,128)(2,1)}, bf16[2,4096,256]{2,1,0:T(8,128)(2,1)}) custom-call(bf16[768,4096]{1,0:T(8,128)(2,1)} %bitcast.8, f32[768,128]{1,0:T(8,128)} %get-tuple-element.12.cos_ref, f32[768,128]{1,0:T(8,128)} %get-tuple-element.13.sin_ref, bf16[4096,4096]{1,0:T(8,128)(2,1)} %wq_ref.1, bf16[4096,1024]{1,0:T(8,128)(2,1)} %wk_ref.1, ...), custom_call_target="tpu_custom_call" | custom-call | tf_op jit(solution)/shard_map/project_and_send/pallas_call | solution.py:285
  160.1 119.6 %attend_and_return.1 = bf16[6,128,4096]{2,1,0:T(8,128)(2,1)} custom-call(bf16[3,4096,256]{2,1,0:T(8,128)(2,1)} %get-tuple-element.7.q_ref, bf16[2,4096,256]{2,1,0:T(8,128)(2,1)} %get-tuple-element.8.kv_ref), custom_call_target="tpu_custom_call" | custom-call | tf_op jit(solution)/shard_map/attend_and_return/pallas_call | solution.py:306
  279.7 33.5 %fusion.3 = bf16[6,128,4096]{2,1,0:T(8,128)(2,1)} fusion(bf16[6,128,4096]{2,1,0:T(8,128)(2,1)} %param.7, bf16[6,128,4096]{2,1,0:T(8,128)(2,1)} %attend_and_return.1, bf16[4096,4096,1]{1,0,2:T(8,128)(2,1)} %bitcast.9), kind=kOutput, calls=%fused_computation.6 | convolution fusion | flops 25779240960 | bytes 52428800 | tf_op jit(solution)/shard_map/bqe,ed->bqd/dot_general | solution.py:324
  (2 shorter events, 0.0 us)
Async XLA Ops:
  0.0 8.4 %copy-start = (bf16[6,128,4096]{2,1,0:T(8,128)(2,1)S(1)}, bf16[6,128,4096]{2,1,0:T(8,128)(2,1)}, u32[]{:S(2)}) copy-start(bf16[6,128,4096]{2,1,0:T(8,128)(2,1)} %param.7) | copy-start | bytes 18874372

commit v3 on v1

v3 whole, which is shorter than its diff:
```python
import functools

import jax
import jax.numpy as jnp
from jax import lax
from jax.experimental import pallas as pl
from jax.experimental.pallas import tpu as pltpu
from jax.sharding import PartitionSpec as P

AXIS = 'cp'
LOG2E = 1.4426950408889634
CHUNK = 32
VMEM_LIMIT = 60 * 1024 * 1024


def rms_norm(hidden, norm_gain):
    x_f32 = hidden.astype(jnp.float32)
    inv_rms = lax.rsqrt(jnp.mean(x_f32 * x_f32, axis=-1, keepdims=True) + 1e-5)
    return (x_f32 * inv_rms * norm_gain.astype(jnp.float32)).astype(jnp.bfloat16)


def rotary_tables(positions, head_dim):
    half_dim = head_dim // 2
    inv_freq = 10000.0 ** (-2.0 * jnp.arange(half_dim, dtype=jnp.float32) / head_dim)
    angles = positions.astype(jnp.float32)[:, :, None] * inv_freq
    cos_part, sin_part = jnp.cos(angles), jnp.sin(angles)
    cos_tab = jnp.concatenate([cos_part, cos_part], axis=-1)
    sin_tab = jnp.concatenate([-sin_part, sin_part], axis=-1)
    return cos_tab.reshape(-1, head_dim), sin_tab.reshape(-1, head_dim)


def group_barrier(me, n_cp):
    barrier = pltpu.get_barrier_semaphore()

    def signal(k, _):
        pl.semaphore_signal(barrier, inc=1, device_id={AXIS: lax.rem(me + k, n_cp)}, device_id_type=pl.DeviceIdType.MESH)
        return 0

    lax.fori_loop(1, n_cp, signal, 0)
    pl.semaphore_wait(barrier, n_cp - 1)


def put(src, dst, owner, me, send_sem, recv_sem):
    @pl.when(owner == me)
    def _():
        pltpu.make_async_copy(src, dst, recv_sem).start()

    @pl.when(owner != me)
    def _():
        pltpu.make_async_remote_copy(src, dst, send_sem, recv_sem, device_id={AXIS: owner}, device_id_type=pl.DeviceIdType.MESH).start()


def wait_bytes_of(ref, sem):
    pltpu.make_async_copy(ref, ref, sem).wait()


def block_kernel(
    n_cp, h_ref, cos_ref, sin_ref, wq_ref, wk_ref, wv_ref, wo_ref, x_ref, y_ref,
    w_buf, acc, stage, q_in, kv_in, v_t, o_stage, s_buf, p_buf, o_acc, stat, o_in, x_buf, y_buf,
    w_sem, x_sem, y_sem, send_q, send_kv, send_o, send_half, recv_q, recv_kv, recv_o, recv_half,
):
    me = lax.axis_index(AXIS)
    chip, core = me // 2, lax.rem(me, 2)
    n_steps, batch, seq, width = stage.shape
    rounds, total, _ = q_in.shape
    per_round = batch // rounds
    n_q = n_cp // per_round
    n_kv = n_steps - n_q
    head_dim = width // 2
    half_dim = head_dim // 2
    blk_q = s_buf.shape[1] // 2
    blk_k = s_buf.shape[0]
    n_blocks = total // blk_q
    ratio = blk_k // blk_q
    span = blk_q // seq
    chips_per_k = blk_k // (2 * seq)
    factor = LOG2E * head_dim ** -0.5

    def kv_block(step):
        return lax.rem(step + chip, n_kv)

    def q_block(step):
        return lax.rem(step - n_kv + chip, n_q)

    def fetch(step, slot):
        @pl.when(step < n_kv)
        def _():
            cols = pl.ds(pl.multiple_of(kv_block(step) * head_dim, head_dim), head_dim)
            pltpu.make_async_copy(wk_ref.at[:, cols], w_buf.at[slot, :, pl.ds(0, head_dim)], w_sem.at[slot]).start()
            pltpu.make_async_copy(wv_ref.at[:, cols], w_buf.at[slot, :, pl.ds(head_dim, head_dim)], w_sem.at[slot]).start()

        @pl.when(step >= n_kv)
        def _():
            cols = pl.ds(pl.multiple_of(q_block(step) * width, width), width)
            pltpu.make_async_copy(wq_ref.at[:, cols], w_buf.at[slot], w_sem.at[slot]).start()

    def send_kv_tiles(step):
        for b in range(batch):
            owner = 2 * (b % per_round * n_kv + kv_block(step)) + core
            r = b // per_round
            put(stage.at[step, b], kv_in.at[r, chip, core], owner, me, send_kv, recv_kv.at[r])

    def send_q_tiles(step, r):
        for k in range(per_round):
            put(stage.at[step, r * per_round + k], q_in.at[r, pl.ds(me * seq, seq)], k * n_q + q_block(step), me, send_q, recv_q.at[r])

    def send_first(step):
        @pl.when(step < n_kv)
        def _():
            send_kv_tiles(step)

        @pl.when(step >= n_kv)
        def _():
            send_q_tiles(step, 0)

    fetch(0, 0)
    group_barrier(me, n_cp)

    def rotate(x):
        return (x * cos_ref[...] + pltpu.roll(x, half_dim, 1) * sin_ref[...]).astype(jnp.bfloat16).reshape(batch, seq, head_dim)

    def project(step, _):
        slot = lax.rem(step, 2)
        wait_bytes_of(w_buf.at[slot], w_sem.at[slot])

        @pl.when(step + 1 < n_steps)
        def _():
            fetch(step + 1, 1 - slot)

        acc[...] = jnp.dot(h_ref[...], w_buf[slot], preferred_element_type=jnp.float32)
        stage[step, :, :, 0:head_dim] = rotate(acc[:, 0:head_dim])

        @pl.when(step < n_kv)
        def _():
            stage[step, :, :, head_dim:width] = acc[:, head_dim:width].astype(jnp.bfloat16).reshape(batch, seq, head_dim)

        @pl.when(step >= n_kv)
        def _():
            stage[step, :, :, head_dim:width] = rotate(acc[:, head_dim:width])

        @pl.when(step > 0)
        def _():
            send_first(step - 1)

        return 0

    lax.fori_loop(0, n_steps, project, 0)
    send_first(n_steps - 1)

    def send_rest(k, _):
        send_q_tiles(n_kv + lax.rem(k, n_q), 1 + k // n_q)
        return 0

    lax.fori_loop(0, (rounds - 1) * n_q, send_rest, 0)

    def out_fetch(k, slot):
        r, cols = k // n_out, pl.ds(pl.multiple_of(lax.rem(k, n_out) * width, width), width)
        pltpu.make_async_copy(wo_ref.at[:, cols], w_buf.at[slot], w_sem.at[slot]).start()
        pltpu.make_async_copy(x_ref.at[pl.ds(r * per_round, per_round), :, cols], x_buf.at[slot], x_sem.at[slot]).start()

    n_out = wo_ref.shape[1] // width
    out_fetch(0, 0)

    def place(t):
        i = lax.rem(t + chip + 1, n_blocks)
        return i, i // ratio

    def attend(r, _):
        wait_bytes_of(kv_in.at[r, :, 0], recv_kv.at[r])
        mine = kv_in.at[r, :, core]
        pltpu.make_async_remote_copy(mine, mine, send_half, recv_half.at[r], device_id={AXIS: me + 1 - 2 * core}, device_id_type=pl.DeviceIdType.MESH).start()
        wait_bytes_of(q_in.at[r], recv_q.at[r])
        wait_bytes_of(kv_in.at[r, :, 0], recv_half.at[r])

        def kv_rows(j, lanes):
            return kv_in[r, pl.ds(j * chips_per_k, chips_per_k), :, :, lanes].reshape(blk_k, head_dim)

        def turn(j, _):
            v_t[:, pl.ds(pl.multiple_of(j * blk_k, blk_k), blk_k)] = kv_rows(j, slice(head_dim, width)).astype(jnp.float32).T.astype(jnp.bfloat16)
            return 0

        lax.fori_loop(0, total // blk_k, turn, 0)

        def send(t):
            i, _ = place(t)
            b = r * per_round + me // n_q
            cols = pl.ds(pl.multiple_of(lax.rem(me, n_q) * width, width), width)
            for s in range(span):
                owner = i * span + s
                put(o_stage.at[r, pl.ds(owner * seq, seq)], o_in.at[b, :, cols], owner, me, send_o, recv_o.at[r])

        def next_scores(i, j):
            k_blk = kv_rows(j, slice(0, head_dim))
            q_rows = pl.ds(pl.multiple_of(i * blk_q, blk_q), blk_q)
            for g in range(2):
                q_head = q_in[r, q_rows, g * head_dim:(g + 1) * head_dim]
                cols = slice(g * blk_q, (g + 1) * blk_q)
                s = lax.dot_general(k_blk, q_head, (((1,), (1,)), ((), ())), preferred_element_type=jnp.float32)
                s_buf[:, cols] = s
                stat[3, 0:1, cols] = jnp.max(s, axis=0, keepdims=True)

        def weighed(j):
            cols = pl.ds(pl.multiple_of(j * blk_k, blk_k), blk_k)
            return o_acc[...] * stat[2, 0:1, :] + jnp.dot(v_t[:, cols], p_buf[...], preferred_element_type=jnp.float32)

        def finish(t):
            i, n_full = place(t)
            out = weighed(jnp.maximum(n_full - 1, 0)) * (1.0 / stat[1, 0:1, :])
            q_rows = pl.ds(pl.multiple_of(i * blk_q, blk_q), blk_q)
            for g in range(2):
                o_stage[r, q_rows, g * head_dim:(g + 1) * head_dim] = out[:, g * blk_q:(g + 1) * blk_q].T.astype(jnp.bfloat16)

        def step(t, _):
            i, n_full = place(t)
            after = place(jnp.minimum(t + 1, n_blocks - 1))

            def follow(n_done):
                more = n_done < n_full
                next_scores(jnp.where(more, i, after[0]), jnp.where(more, n_done, after[1]))

            @pl.when(t > 1)
            def _():
                send(t - 2)

            def diagonal(size):
                finish(jnp.maximum(t - 1, 0))
                o_acc[...] = jnp.zeros_like(o_acc)
                shape = (size, 2 * blk_q)
                allowed = lax.broadcasted_iota(jnp.int32, shape, 0) - (size - blk_q) <= lax.rem(lax.broadcasted_iota(jnp.int32, shape, 1), blk_q)
                s = jnp.where(allowed, s_buf[0:size, :], -jnp.inf)
                top = jnp.max(s, axis=0, keepdims=True)
                prob = jnp.exp2(s * factor - top * factor)
                stat[0, 0:1, :] = top
                stat[1, 0:1, :] = jnp.sum(prob, axis=0, keepdims=True)
                stat[2, 0:1, :] = jnp.ones_like(top)
                p_buf[0:size, :] = prob.astype(jnp.bfloat16)
                if size < blk_k:
                    p_buf[size:blk_k, :] = jnp.zeros((blk_k - size, 2 * blk_q), jnp.bfloat16)
                follow(0)

            for part in range(ratio):
                pl.when(lax.rem(i, ratio) == part)(functools.partial(diagonal, (part + 1) * blk_q))

            def full(j, _):
                o_acc[...] = weighed(jnp.where(j == 0, n_full, j - 1))
                top = stat[0, 0:1, :]
                new_top = jnp.maximum(top, stat[3, 0:1, :])
                shift = new_top * factor
                rescale = jnp.exp2(top * factor - shift)
                part_sum = jnp.zeros((8, 2 * blk_q), jnp.float32)
                for k in range(0, blk_k, CHUNK):
                    prob = jnp.exp2(s_buf[k:k + CHUNK, :] * factor - shift)
                    part_sum = part_sum + jnp.sum(prob.reshape(CHUNK // 8, 8, 2 * blk_q), axis=0)
                    p_buf[k:k + CHUNK, :] = prob.astype(jnp.bfloat16)
                stat[0, 0:1, :] = new_top
                stat[1, 0:1, :] = stat[1, 0:1, :] * rescale + jnp.sum(part_sum, axis=0, keepdims=True)
                stat[2, 0:1, :] = rescale
                follow(j + 1)
                return 0

            lax.fori_loop(0, n_full, full, 0)
            return 0

        o_acc[...] = jnp.zeros_like(o_acc)
        stat[...] = jnp.ones_like(stat)
        p_buf[...] = jnp.zeros_like(p_buf)
        next_scores(*place(0))
        lax.fori_loop(0, n_blocks, step, 0)
        send(n_blocks - 2)
        finish(n_blocks - 1)
        send(n_blocks - 1)
        return 0

    lax.fori_loop(0, rounds, attend, 0)

    def y_copy(k, slot):
        r, cols = k // n_out, pl.ds(pl.multiple_of(lax.rem(k, n_out) * width, width), width)
        return pltpu.make_async_copy(y_buf.at[slot], y_ref.at[pl.ds(r * per_round, per_round), :, cols], y_sem.at[slot])

    def out_project(k, _):
        slot, r = lax.rem(k, 2), k // n_out

        @pl.when(k + 1 < rounds * n_out)
        def _():
            out_fetch(k + 1, 1 - slot)

        @pl.when(lax.rem(k, n_out) == 0)
        def _():
            wait_bytes_of(o_in.at[pl.ds(r * per_round, per_round)], recv_o.at[r])

        wait_bytes_of(w_buf.at[slot], w_sem.at[slot])
        wait_bytes_of(x_buf.at[slot], x_sem.at[slot])

        @pl.when(k > 1)
        def _():
            y_copy(k - 2, slot).wait()

        attn = o_in[pl.ds(r * per_round, per_round)].reshape(per_round * seq, wo_ref.shape[0])
        proj = jnp.dot(attn, w_buf[slot], preferred_element_type=jnp.float32)
        y_buf[slot] = (x_buf[slot].astype(jnp.float32) + proj.reshape(per_round, seq, width)).astype(jnp.bfloat16)
        y_copy(k, slot).start()
        return 0

    lax.fori_loop(0, rounds * n_out, out_project, 0)
    for k in (rounds * n_out - 2, rounds * n_out - 1):
        y_copy(k, k % 2).wait()
    away = (n_cp - 1) * seq
    wait_bytes_of(q_in.at[:, pl.ds(0, away)], send_q)
    wait_bytes_of(kv_in.at[:, pl.ds(0, n_cp // 2 - 1), 0], send_kv)
    wait_bytes_of(o_stage.at[:, pl.ds(0, away)], send_o)
    wait_bytes_of(kv_in.at[:, :, 0], send_half)


def solution(mesh):
    n_cp = mesh.shape[AXIS]

    def local_block(hidden, positions, norm_gain, w_query, w_key, w_value, w_out):
        batch, seq, model_dim = hidden.shape
        n_heads, head_dim, _ = w_out.shape
        n_kv = w_key.shape[1] // head_dim
        width = 2 * head_dim
        n_q = n_heads // 2
        rounds = batch * n_q // n_cp
        per_round = batch // rounds
        total = n_cp * seq
        n_steps = n_kv + n_q
        blk_q = 2 * seq
        blk_k = 2 * blk_q
        any_space = pl.BlockSpec(memory_space=pl.ANY)
        vmem = pl.BlockSpec(memory_space=pltpu.VMEM)
        normed = rms_norm(hidden, norm_gain).reshape(batch * seq, model_dim)
        cos_tab, sin_tab = rotary_tables(positions, head_dim)
        dma = pltpu.SemaphoreType.DMA
        return pl.pallas_call(
            functools.partial(block_kernel, n_cp),
            out_shape=jax.ShapeDtypeStruct(hidden.shape, jnp.bfloat16),
            in_specs=[vmem, vmem, vmem] + [any_space] * 5,
            out_specs=any_space,
            scratch_shapes=[
                pltpu.VMEM((2, model_dim, width), jnp.bfloat16),
                pltpu.VMEM((batch * seq, width), jnp.float32),
                pltpu.VMEM((n_steps, batch, seq, width), jnp.bfloat16),
                pltpu.VMEM((rounds, total, width), jnp.bfloat16),
                pltpu.VMEM((rounds, n_cp // 2, 2, seq, width), jnp.bfloat16),
                pltpu.VMEM((head_dim, total), jnp.bfloat16),
                pltpu.VMEM((rounds, total, width), jnp.bfloat16),
                pltpu.VMEM((blk_k, 2 * blk_q), jnp.float32),
                pltpu.VMEM((blk_k, 2 * blk_q), jnp.bfloat16),
                pltpu.VMEM((head_dim, 2 * blk_q), jnp.float32),
                pltpu.VMEM((4, 8, 2 * blk_q), jnp.float32),
                pltpu.VMEM((batch, seq, n_heads * head_dim), jnp.bfloat16),
                pltpu.VMEM((2, per_round, seq, width), jnp.bfloat16),
                pltpu.VMEM((2, per_round, seq, width), jnp.bfloat16),
                dma((2,)), dma((2,)), dma((2,)),
                dma, dma, dma, dma,
                dma((rounds,)), dma((rounds,)), dma((rounds,)), dma((rounds,)),
            ],
            compiler_params=pltpu.CompilerParams(collective_id=0, has_side_effects=True, vmem_limit_bytes=VMEM_LIMIT),
            name='attention_block',
        )(normed, cos_tab, sin_tab, w_query, w_key, w_value, w_out.reshape(n_heads * head_dim, model_dim), hidden)

    act_spec = P('dp', 'cp', None)
    return jax.shard_map(local_block, mesh=mesh, in_specs=(act_spec, P('dp', 'cp'), P(), P(), P(), P(), P()), out_specs=act_spec, check_vma=False)
```

time: 391 us -> 273 us (0.70)
  the two profiles are of different devices: /device:TPU:97 before, /device:TPU:105 now
where the time goes in v3:
time: 273 us; the launch traced here: 272 us
  Pallas kernels  252 us (92%)
  other arithmetic  13.8 us (5%)
  local copies, waits for them, and re-layouts  6.29 us (2%)
    pallas_call x1, Pallas kernels, local_block(): pl.pallas_call(functools.partial(block_kernel, n_cp), out_shape=jax.Shape...  252 us
    unnamed x3, local copies, waits for them, and re-layouts  6.29 us

profile of v3, /device:TPU:105, one launch (start us, length us, event | category | flops | bytes accessed | tf_op | source)
XLA Modules:
  0.0 271.6 jit_solution(15267065418159175354)
XLA Ops:
  0.0 0.0 copy-start
  0.0 0.8 convert_bitcast_fusion
  0.9 4.2 %fusion = f32[6,128]{1,0:T(8,128)S(1)} fusion(bf16[6,128,4096]{2,1,0:T(8,128)(2,1)} %x_ref.1), kind=kLoop, calls=%fused_computation.2 | loop fusion | flops 9436416 | bytes 6294528 | tf_op jit(solution)/shard_map/reduce_sum | solution.py:18
  5.1 0.7 convert_element_type.13
  5.8 1.4 fusion.3
  7.2 1.2 pad_maximum_fusion
  8.4 0.0 copy-done
  8.4 5.4 %fusion.2 = bf16[6,128,4096]{2,1,0:T(8,128)(2,1)} fusion(bf16[6,128,4096]{2,1,0:T(8,128)(2,1)S(1)} %copy-done, f32[4096]{0:T(1024)S(1)} %convert_element_type.13, f32[6,128]{1,0:T(8,128)S(1)} %add_rsqrt_fusion), kind=kLoop, calls=%fused_computation.4 | loop fusion | flops 12582912 | bytes 12602368 | tf_op jit(solution)/shard_map/convert_element_type | solution.py:19
  13.8 251.5 %attention_block.1 = bf16[6,128,4096]{2,1,0:T(8,128)(2,1)} custom-call(bf16[768,4096]{1,0:T(8,128)(2,1)} %bitcast.5, f32[768,128]{1,0:T(8,128)} %get-tuple-element.8.cos_ref, f32[768,128]{1,0:T(8,128)} %get-tuple-element.9.sin_ref, bf16[4096,4096]{1,0:T(8,128)(2,1)} %wq_ref.1, bf16[4096,1024]{1,0:T(8,128)(2,1)} %wk_ref.1, bf16[4096,1024]{1,0:T(8,128)(2,1)} %wv_ref.1, ...), custom_call_target="tpu_custom_call" | custom-call | tf_op jit(solution)/shard_map/attention_block/pallas_call | solution.py:334
  265.3 6.3 %copy.9 = bf16[6,128,4096]{2,1,0:T(8,128)(2,1)} copy(bf16[6,128,4096]{2,1,0:T(8,128)(2,1)} %attention_block.1) | data formatting | bytes 12582912
  (2 shorter events, 0.0 us)
Async XLA Ops:
  0.0 8.4 %copy-start = (bf16[6,128,4096]{2,1,0:T(8,128)(2,1)S(1)}, bf16[6,128,4096]{2,1,0:T(8,128)(2,1)}, u32[]{:S(2)}) copy-start(bf16[6,128,4096]{2,1,0:T(8,128)(2,1)} %x_ref.1) | copy-start | bytes 18874372

commit v4 on v3

--- a/solution.py
+++ b/solution.py
@@ -10,26 +10,33 @@
 AXIS = 'cp'
 LOG2E = 1.4426950408889634
 CHUNK = 32
+NORM_ROWS = 32
 VMEM_LIMIT = 60 * 1024 * 1024
 
 
-def rms_norm(hidden, norm_gain):
-    x_f32 = hidden.astype(jnp.float32)
-    inv_rms = lax.rsqrt(jnp.mean(x_f32 * x_f32, axis=-1, keepdims=True) + 1e-5)
-    return (x_f32 * inv_rms * norm_gain.astype(jnp.float32)).astype(jnp.bfloat16)
+def cos_sin(angles):
+    quarter = jnp.round(angles * 0.6366197723675814)
+    rest = ((angles - quarter * 1.5703125) - quarter * 4.837512969970703e-4) - quarter * 7.549789954891626e-8
+    square = rest * rest
+    sin_poly = rest + rest * square * (-1.6666654611e-1 + square * (8.3321608736e-3 - square * 1.9515295891e-4))
+    cos_poly = 1.0 - 0.5 * square + square * square * (4.166664568298827e-2 + square * (-1.388731625493765e-3 + square * 2.443315711809948e-5))
+    turn = quarter.astype(jnp.int32) & 3
+    odd = (turn & 1) == 1
+    cos_part = jnp.where(odd, sin_poly, cos_poly)
+    sin_part = jnp.where(odd, cos_poly, sin_poly)
+    return jnp.where((turn == 1) | (turn == 2), -cos_part, cos_part), jnp.where(turn >= 2, -sin_part, sin_part)
 
 
 def rotary_tables(positions, head_dim):
     half_dim = head_dim // 2
     inv_freq = 10000.0 ** (-2.0 * jnp.arange(half_dim, dtype=jnp.float32) / head_dim)
-    angles = positions.astype(jnp.float32)[:, :, None] * inv_freq
-    cos_part, sin_part = jnp.cos(angles), jnp.sin(angles)
-    cos_tab = jnp.concatenate([cos_part, cos_part], axis=-1)
-    sin_tab = jnp.concatenate([-sin_part, sin_part], axis=-1)
-    return cos_tab.reshape(-1, head_dim), sin_tab.reshape(-1, head_dim)
-
-
-def group_barrier(me, n_cp):
+    sign = jnp.where(jnp.arange(head_dim) < half_dim, -1.0, 1.0).astype(jnp.float32)
+    angles = positions.reshape(-1, 1).astype(jnp.float32) * jnp.concatenate([inv_freq, inv_freq])
+    cos_tab, sin_tab = cos_sin(angles)
+    return cos_tab, sin_tab * sign
+
+
+def group_signal(me, n_cp):
     barrier = pltpu.get_barrier_semaphore()
 
     def signal(k, _):
@@ -37,7 +44,6 @@
         return 0
 
     lax.fori_loop(1, n_cp, signal, 0)
-    pl.semaphore_wait(barrier, n_cp - 1)
 
 
 def put(src, dst, owner, me, send_sem, recv_sem):
@@ -55,9 +61,9 @@
 
 
 def block_kernel(
-    n_cp, h_ref, cos_ref, sin_ref, wq_ref, wk_ref, wv_ref, wo_ref, x_ref, y_ref,
-    w_buf, acc, stage, q_in, kv_in, v_t, o_stage, s_buf, p_buf, o_acc, stat, o_in, x_buf, y_buf,
-    w_sem, x_sem, y_sem, send_q, send_kv, send_o, send_half, recv_q, recv_kv, recv_o, recv_half,
+    n_cp, x_ref, gain_ref, cos_ref, sin_ref, wq_ref, wk_ref, wv_ref, wo_ref, y_ref,
+    h_ref, w_buf, acc, stage, q_in, kv_in, v_t, o_stage, s_buf, p_buf, o_acc, stat, o_in, y_buf,
+    w_sem, y_sem, send_q, send_kv, send_o, send_half, recv_q, recv_kv, recv_o, recv_half,
 ):
     me = lax.axis_index(AXIS)
     chip, core = me // 2, lax.rem(me, 2)
@@ -114,7 +120,17 @@
             send_q_tiles(step, 0)
 
     fetch(0, 0)
-    group_barrier(me, n_cp)
+    group_signal(me, n_cp)
+
+    def norm(k, _):
+        rows = pl.ds(pl.multiple_of(k * NORM_ROWS, NORM_ROWS), NORM_ROWS)
+        x = x_ref[rows, :].astype(jnp.float32)
+        inv_rms = lax.rsqrt(jnp.mean(x * x, axis=-1, keepdims=True) + 1e-5)
+        h_ref[rows, :] = (x * inv_rms * gain_ref[...].astype(jnp.float32)).astype(jnp.bfloat16)
+        return 0
+
+    lax.fori_loop(0, batch * seq // NORM_ROWS, norm, 0)
+    pl.semaphore_wait(pltpu.get_barrier_semaphore(), n_cp - 1)
 
     def rotate(x):
         return (x * cos_ref[...] + pltpu.roll(x, half_dim, 1) * sin_ref[...]).astype(jnp.bfloat16).reshape(batch, seq, head_dim)
@@ -147,6 +163,14 @@
     lax.fori_loop(0, n_steps, project, 0)
     send_first(n_steps - 1)
 
+    def swap(r, _):
+        wait_bytes_of(kv_in.at[r, :, 0], recv_kv.at[r])
+        mine = kv_in.at[r, :, core]
+        pltpu.make_async_remote_copy(mine, mine, send_half, recv_half.at[r], device_id={AXIS: me + 1 - 2 * core}, device_id_type=pl.DeviceIdType.MESH).start()
+        return 0
+
+    lax.fori_loop(0, rounds, swap, 0)
+
     def send_rest(k, _):
         send_q_tiles(n_kv + lax.rem(k, n_q), 1 + k // n_q)
         return 0
@@ -154,9 +178,8 @@
     lax.fori_loop(0, (rounds - 1) * n_q, send_rest, 0)
 
     def out_fetch(k, slot):
-        r, cols = k // n_out, pl.ds(pl.multiple_of(lax.rem(k, n_out) * width, width), width)
+        cols = pl.ds(pl.multiple_of(lax.rem(k, n_out) * width, width), width)
         pltpu.make_async_copy(wo_ref.at[:, cols], w_buf.at[slot], w_sem.at[slot]).start()
-        pltpu.make_async_copy(x_ref.at[pl.ds(r * per_round, per_round), :, cols], x_buf.at[slot], x_sem.at[slot]).start()
 
     n_out = wo_ref.shape[1] // width
     out_fetch(0, 0)
@@ -166,9 +189,6 @@
         return i, i // ratio
 
     def attend(r, _):
-        wait_bytes_of(kv_in.at[r, :, 0], recv_kv.at[r])
-        mine = kv_in.at[r, :, core]
-        pltpu.make_async_remote_copy(mine, mine, send_half, recv_half.at[r], device_id={AXIS: me + 1 - 2 * core}, device_id_type=pl.DeviceIdType.MESH).start()
         wait_bytes_of(q_in.at[r], recv_q.at[r])
         wait_bytes_of(kv_in.at[r, :, 0], recv_half.at[r])
 
@@ -289,7 +309,6 @@
             wait_bytes_of(o_in.at[pl.ds(r * per_round, per_round)], recv_o.at[r])
 
         wait_bytes_of(w_buf.at[slot], w_sem.at[slot])
-        wait_bytes_of(x_buf.at[slot], x_sem.at[slot])
 
         @pl.when(k > 1)
         def _():
@@ -297,7 +316,9 @@
 
         attn = o_in[pl.ds(r * per_round, per_round)].reshape(per_round * seq, wo_ref.shape[0])
         proj = jnp.dot(attn, w_buf[slot], preferred_element_type=jnp.float32)
-        y_buf[slot] = (x_buf[slot].astype(jnp.float32) + proj.reshape(per_round, seq, width)).astype(jnp.bfloat16)
+        rows = pl.ds(pl.multiple_of(r * per_round * seq, seq), per_round * seq)
+        cols = pl.ds(pl.multiple_of(lax.rem(k, n_out) * width, width), width)
+        y_buf[slot] = (x_ref[rows, cols].astype(jnp.float32) + proj).astype(jnp.bfloat16).reshape(per_round, seq, width)
         y_copy(k, slot).start()
         return 0
 
@@ -328,15 +349,15 @@
         blk_k = 2 * blk_q
         any_space = pl.BlockSpec(memory_space=pl.ANY)
         vmem = pl.BlockSpec(memory_space=pltpu.VMEM)
-        normed = rms_norm(hidden, norm_gain).reshape(batch * seq, model_dim)
         cos_tab, sin_tab = rotary_tables(positions, head_dim)
         dma = pltpu.SemaphoreType.DMA
         return pl.pallas_call(
             functools.partial(block_kernel, n_cp),
             out_shape=jax.ShapeDtypeStruct(hidden.shape, jnp.bfloat16),
-            in_specs=[vmem, vmem, vmem] + [any_space] * 5,
+            in_specs=[vmem] * 4 + [any_space] * 4,
             out_specs=any_space,
             scratch_shapes=[
+                pltpu.VMEM((batch * seq, model_dim), jnp.bfloat16),
                 pltpu.VMEM((2, model_dim, width), jnp.bfloat16),
                 pltpu.VMEM((batch * seq, width), jnp.float32),
                 pltpu.VMEM((n_steps, batch, seq, width), jnp.bfloat16),
@@ -350,14 +371,13 @@
                 pltpu.VMEM((4, 8, 2 * blk_q), jnp.float32),
                 pltpu.VMEM((batch, seq, n_heads * head_dim), jnp.bfloat16),
                 pltpu.VMEM((2, per_round, seq, width), jnp.bfloat16),
-                pltpu.VMEM((2, per_round, seq, width), jnp.bfloat16),
-                dma((2,)), dma((2,)), dma((2,)),
+                dma((2,)), dma((2,)),
                 dma, dma, dma, dma,
                 dma((rounds,)), dma((rounds,)), dma((rounds,)), dma((rounds,)),
             ],
             compiler_params=pltpu.CompilerParams(collective_id=0, has_side_effects=True, vmem_limit_bytes=VMEM_LIMIT),
             name='attention_block',
-        )(normed, cos_tab, sin_tab, w_query, w_key, w_value, w_out.reshape(n_heads * head_dim, model_dim), hidden)
+        )(hidden.reshape(batch * seq, model_dim), norm_gain.reshape(1, model_dim), cos_tab, sin_tab, w_query, w_key, w_value, w_out.reshape(n_heads * head_dim, model_dim))
 
     act_spec = P('dp', 'cp', None)
     return jax.shard_map(local_block, mesh=mesh, in_specs=(act_spec, P('dp', 'cp'), P(), P(), P(), P(), P()), out_specs=act_spec, check_vma=False)

time: 273 us -> 261 us (0.956)
  other arithmetic: 13.8 us -> 2.24 us
    convert_element_type x2 -> x1, other arithmetic: 6.12 us -> 0.69 us  [rotary_tables(): positions.reshape(-1, 1).astype(jnp.float32)]
    reduce_sum x1 -> x0, other arithmetic: 4.22 us -> none  [rms_norm(): inv_rms = lax.rsqrt(jnp.mean(x_f32 * x_f32, axis=-1, keepdims=True) + 1e-05)]
    unnamed x3 -> x1, local copies, waits for them, and re-layouts: 6.29 us -> 6.29 us
where the time goes in v4:
time: 261 us; the launch traced here: 260 us
  Pallas kernels  250 us (96%)
  local copies, waits for them, and re-layouts  7.6 us (3%)
    pallas_call x1, Pallas kernels, local_block(): pl.pallas_call(functools.partial(block_kernel, n_cp), out_shape=jax.Shape...  250 us
    unnamed x1, local copies, waits for them, and re-layouts  6.29 us

profile of v4, /device:TPU:105, one launch (start us, length us, event | category | flops | bytes accessed | tf_op | source)
XLA Modules:
  0.0 259.7 jit_solution(8705143260933911908)
XLA Ops:
  0.0 0.1 compare_select_fusion
  0.1 0.7 convert_bitcast_fusion
  0.8 1.3 reshape.25.gain_ref
  2.1 1.5 fusion.22
  3.6 249.8 %attention_block.1 = bf16[6,128,4096]{2,1,0:T(8,128)(2,1)} custom-call(bf16[768,4096]{1,0:T(8,128)(2,1)} %bitcast.5, bf16[1,4096]{1,0:T(2,128)(2,1)} %reshape.25.gain_ref, f32[768,128]{1,0:T(8,128)} %get-tuple-element.6.cos_ref, f32[768,128]{1,0:T(8,128)} %get-tuple-element.5.sin_ref, bf16[4096,4096]{1,0:T(8,128)(2,1)} %wq_ref.1, bf16[4096,1024]{1,0:T(8,128)(2,1)} %wk_ref.1, ...), custom_call_target="tpu_custom_call" | custom-call | tf_op jit(solution)/shard_map/attention_block/pallas_call | solution.py:354
  253.4 6.3 %copy.9 = bf16[6,128,4096]{2,1,0:T(8,128)(2,1)} copy(bf16[6,128,4096]{2,1,0:T(8,128)(2,1)} %attention_block.1) | data formatting | bytes 12582912
  (1 shorter events, 0.0 us)

commit v5 on v4

--- a/solution.py
+++ b/solution.py
@@ -100,8 +100,8 @@
             cols = pl.ds(pl.multiple_of(q_block(step) * width, width), width)
             pltpu.make_async_copy(wq_ref.at[:, cols], w_buf.at[slot], w_sem.at[slot]).start()
 
-    def send_kv_tiles(step):
-        for b in range(batch):
+    def send_kv_tiles(step, first, last):
+        for b in range(first * per_round, last * per_round):
             owner = 2 * (b % per_round * n_kv + kv_block(step)) + core
             r = b // per_round
             put(stage.at[step, b], kv_in.at[r, chip, core], owner, me, send_kv, recv_kv.at[r])
@@ -110,10 +110,12 @@
         for k in range(per_round):
             put(stage.at[step, r * per_round + k], q_in.at[r, pl.ds(me * seq, seq)], k * n_q + q_block(step), me, send_q, recv_q.at[r])
 
+    early = min(2, rounds)
+
     def send_first(step):
         @pl.when(step < n_kv)
         def _():
-            send_kv_tiles(step)
+            send_kv_tiles(step, 0, early)
 
         @pl.when(step >= n_kv)
         def _():
@@ -169,10 +171,15 @@
         pltpu.make_async_remote_copy(mine, mine, send_half, recv_half.at[r], device_id={AXIS: me + 1 - 2 * core}, device_id_type=pl.DeviceIdType.MESH).start()
         return 0
 
-    lax.fori_loop(0, rounds, swap, 0)
+    lax.fori_loop(0, early, swap, 0)
 
     def send_rest(k, _):
         send_q_tiles(n_kv + lax.rem(k, n_q), 1 + k // n_q)
+
+        @pl.when(k < n_kv)
+        def _():
+            send_kv_tiles(k, early, rounds)
+
         return 0
 
     lax.fori_loop(0, (rounds - 1) * n_q, send_rest, 0)
@@ -185,10 +192,14 @@
     out_fetch(0, 0)
 
     def place(t):
-        i = lax.rem(t + chip + 1, n_blocks)
+        i = lax.rem(t + me // span + 1, n_blocks)
         return i, i // ratio
 
     def attend(r, _):
+        @pl.when((r + 1 >= early) & (r + 1 < rounds))
+        def _():
+            swap(r + 1, 0)
+
         wait_bytes_of(q_in.at[r], recv_q.at[r])
         wait_bytes_of(kv_in.at[r, :, 0], recv_half.at[r])
 
@@ -345,8 +356,8 @@
         per_round = batch // rounds
         total = n_cp * seq
         n_steps = n_kv + n_q
-        blk_q = 2 * seq
-        blk_k = 2 * blk_q
+        blk_q = 4 * seq
+        blk_k = blk_q
         any_space = pl.BlockSpec(memory_space=pl.ANY)
         vmem = pl.BlockSpec(memory_space=pltpu.VMEM)
         cos_tab, sin_tab = rotary_tables(positions, head_dim)

time: 261 us -> 255 us (0.977)
  the two profiles are of different devices: /device:TPU:105 before, /device:TPU:97 now
where the time goes in v5:
time: 255 us; the launch traced here: 254 us
  Pallas kernels  244 us (96%)
  local copies, waits for them, and re-layouts  7.6 us (3%)
    pallas_call x1, Pallas kernels, local_block(): pl.pallas_call(functools.partial(block_kernel, n_cp), out_shape=jax.Shape...  244 us
    unnamed x1, local copies, waits for them, and re-layouts  6.29 us

profile of v5, /device:TPU:97, one launch (start us, length us, event | category | flops | bytes accessed | tf_op | source)
XLA Modules:
  0.0 253.5 jit_solution(5483667321311418829)
XLA Ops:
  0.0 0.1 compare_select_fusion
  0.1 0.7 convert_bitcast_fusion
  0.8 1.3 reshape.25.gain_ref
  2.1 1.5 fusion.22
  3.6 243.7 %attention_block.1 = bf16[6,128,4096]{2,1,0:T(8,128)(2,1)} custom-call(bf16[768,4096]{1,0:T(8,128)(2,1)} %bitcast.5, bf16[1,4096]{1,0:T(2,128)(2,1)} %reshape.25.gain_ref, f32[768,128]{1,0:T(8,128)} %get-tuple-element.6.cos_ref, f32[768,128]{1,0:T(8,128)} %get-tuple-element.5.sin_ref, bf16[4096,4096]{1,0:T(8,128)(2,1)} %wq_ref.1, bf16[4096,1024]{1,0:T(8,128)(2,1)} %wk_ref.1, ...), custom_call_target="tpu_custom_call" | custom-call | tf_op jit(solution)/shard_map/attention_block/pallas_call | solution.py:365
  247.2 6.3 %copy.9 = bf16[6,128,4096]{2,1,0:T(8,128)(2,1)} copy(bf16[6,128,4096]{2,1,0:T(8,128)(2,1)} %attention_block.1) | data formatting | bytes 12582912
  (1 shorter events, 0.0 us)

commit v6 on v5

--- a/solution.py
+++ b/solution.py
@@ -31,9 +31,9 @@
     half_dim = head_dim // 2
     inv_freq = 10000.0 ** (-2.0 * jnp.arange(half_dim, dtype=jnp.float32) / head_dim)
     sign = jnp.where(jnp.arange(head_dim) < half_dim, -1.0, 1.0).astype(jnp.float32)
-    angles = positions.reshape(-1, 1).astype(jnp.float32) * jnp.concatenate([inv_freq, inv_freq])
+    angles = positions.astype(jnp.float32)[:, :, None] * jnp.concatenate([inv_freq, inv_freq])
     cos_tab, sin_tab = cos_sin(angles)
-    return cos_tab, sin_tab * sign
+    return cos_tab.reshape(-1, head_dim), (sin_tab * sign).reshape(-1, head_dim)
 
 
 def group_signal(me, n_cp):
@@ -121,6 +121,10 @@
         def _():
             send_q_tiles(step, 0)
 
+        @pl.when((step >= n_kv) & (lax.rem(step, 2) == 1) & ((step - n_kv) // 2 < n_kv))
+        def _():
+            send_kv_tiles((step - n_kv) // 2, early, rounds)
+
     fetch(0, 0)
     group_signal(me, n_cp)
 
@@ -128,7 +132,7 @@
         rows = pl.ds(pl.multiple_of(k * NORM_ROWS, NORM_ROWS), NORM_ROWS)
         x = x_ref[rows, :].astype(jnp.float32)
         inv_rms = lax.rsqrt(jnp.mean(x * x, axis=-1, keepdims=True) + 1e-5)
-        h_ref[rows, :] = (x * inv_rms * gain_ref[...].astype(jnp.float32)).astype(jnp.bfloat16)
+        h_ref[rows, :] = (x * inv_rms * gain_ref[...].astype(jnp.float32).reshape(1, gain_ref.shape[0])).astype(jnp.bfloat16)
         return 0
 
     lax.fori_loop(0, batch * seq // NORM_ROWS, norm, 0)
@@ -175,11 +179,6 @@
 
     def send_rest(k, _):
         send_q_tiles(n_kv + lax.rem(k, n_q), 1 + k // n_q)
-
-        @pl.when(k < n_kv)
-        def _():
-            send_kv_tiles(k, early, rounds)
-
         return 0
 
     lax.fori_loop(0, (rounds - 1) * n_q, send_rest, 0)
@@ -388,7 +387,7 @@
             ],
             compiler_params=pltpu.CompilerParams(collective_id=0, has_side_effects=True, vmem_limit_bytes=VMEM_LIMIT),
             name='attention_block',
-        )(hidden.reshape(batch * seq, model_dim), norm_gain.reshape(1, model_dim), cos_tab, sin_tab, w_query, w_key, w_value, w_out.reshape(n_heads * head_dim, model_dim))
+        )(hidden.reshape(batch * seq, model_dim), norm_gain, cos_tab, sin_tab, w_query, w_key, w_value, w_out.reshape(n_heads * head_dim, model_dim))
 
     act_spec = P('dp', 'cp', None)
     return jax.shard_map(local_block, mesh=mesh, in_specs=(act_spec, P('dp', 'cp'), P(), P(), P(), P(), P()), out_specs=act_spec, check_vma=False)

time: 255 us -> 256 us (level)
  no operation moved by 1% of the time
where the time goes in v6:
time: 256 us; the launch traced here: 254 us
  Pallas kernels  246 us (96%)
  local copies, waits for them, and re-layouts  6.29 us (2%)
    pallas_call x1, Pallas kernels, local_block(): pl.pallas_call(functools.partial(block_kernel, n_cp), out_shape=jax.Shape...  246 us
    unnamed x1, local copies, waits for them, and re-layouts  6.29 us

profile of v6, /device:TPU:97, one launch (start us, length us, event | category | flops | bytes accessed | tf_op | source)
XLA Modules:
  0.0 254.5 jit_solution(2245026603040113116)
XLA Ops:
  0.0 0.1 compare_select_fusion
  0.1 0.7 convert_bitcast_fusion
  0.8 1.5 fusion.22
  2.2 246.0 %attention_block.1 = bf16[6,128,4096]{2,1,0:T(8,128)(2,1)} custom-call(bf16[768,4096]{1,0:T(8,128)(2,1)} %bitcast.5, bf16[4096]{0:T(1024)(128)(2,1)} %gain_ref.1, f32[768,128]{1,0:T(8,128)} %get-tuple-element.6.cos_ref, f32[768,128]{1,0:T(8,128)} %get-tuple-element.5.sin_ref, bf16[4096,4096]{1,0:T(8,128)(2,1)} %wq_ref.1, bf16[4096,1024]{1,0:T(8,128)(2,1)} %wk_ref.1, ...), custom_call_target="tpu_custom_call" | custom-call | tf_op jit(solution)/shard_map/attention_block/pallas_call | solution.py:364
  248.2 6.3 %copy.9 = bf16[6,128,4096]{2,1,0:T(8,128)(2,1)} copy(bf16[6,128,4096]{2,1,0:T(8,128)(2,1)} %attention_block.1) | data formatting | bytes 12582912
  (1 shorter events, 0.0 us)

commit v7 on v5

--- a/solution.py
+++ b/solution.py
@@ -128,7 +128,7 @@
         rows = pl.ds(pl.multiple_of(k * NORM_ROWS, NORM_ROWS), NORM_ROWS)
         x = x_ref[rows, :].astype(jnp.float32)
         inv_rms = lax.rsqrt(jnp.mean(x * x, axis=-1, keepdims=True) + 1e-5)
-        h_ref[rows, :] = (x * inv_rms * gain_ref[...].astype(jnp.float32)).astype(jnp.bfloat16)
+        h_ref[rows, :] = (x * inv_rms * gain_ref[...].astype(jnp.float32).reshape(1, gain_ref.shape[0])).astype(jnp.bfloat16)
         return 0
 
     lax.fori_loop(0, batch * seq // NORM_ROWS, norm, 0)
@@ -388,7 +388,7 @@
             ],
             compiler_params=pltpu.CompilerParams(collective_id=0, has_side_effects=True, vmem_limit_bytes=VMEM_LIMIT),
             name='attention_block',
-        )(hidden.reshape(batch * seq, model_dim), norm_gain.reshape(1, model_dim), cos_tab, sin_tab, w_query, w_key, w_value, w_out.reshape(n_heads * head_dim, model_dim))
+        )(hidden.reshape(batch * seq, model_dim), norm_gain, cos_tab, sin_tab, w_query, w_key, w_value, w_out.reshape(n_heads * head_dim, model_dim))
 
     act_spec = P('dp', 'cp', None)
     return jax.shard_map(local_block, mesh=mesh, in_specs=(act_spec, P('dp', 'cp'), P(), P(), P(), P(), P()), out_specs=act_spec, check_vma=False)

time: 255 us -> 251 us (0.984)
  the two profiles are of different devices: /device:TPU:97 before, /device:TPU:105 now
where the time goes in v7:
time: 251 us; the launch traced here: 250 us
  Pallas kernels  241 us (96%)
  local copies, waits for them, and re-layouts  6.29 us (3%)
    pallas_call x1, Pallas kernels, local_block(): pl.pallas_call(functools.partial(block_kernel, n_cp), out_shape=jax.Shape...  241 us
    unnamed x1, local copies, waits for them, and re-layouts  6.29 us

profile of v7, /device:TPU:105, one launch (start us, length us, event | category | flops | bytes accessed | tf_op | source)
XLA Modules:
  0.0 249.8 jit_solution(581740030437849965)
XLA Ops:
  0.0 0.1 compare_select_fusion
  0.1 0.7 convert_bitcast_fusion
  0.8 1.5 fusion.22
  2.2 241.2 %attention_block.1 = bf16[6,128,4096]{2,1,0:T(8,128)(2,1)} custom-call(bf16[768,4096]{1,0:T(8,128)(2,1)} %bitcast.5, bf16[4096]{0:T(1024)(128)(2,1)} %gain_ref.1, f32[768,128]{1,0:T(8,128)} %get-tuple-element.6.cos_ref, f32[768,128]{1,0:T(8,128)} %get-tuple-element.5.sin_ref, bf16[4096,4096]{1,0:T(8,128)(2,1)} %wq_ref.1, bf16[4096,1024]{1,0:T(8,128)(2,1)} %wk_ref.1, ...), custom_call_target="tpu_custom_call" | custom-call | tf_op jit(solution)/shard_map/attention_block/pallas_call | solution.py:365
  243.5 6.3 %copy.9 = bf16[6,128,4096]{2,1,0:T(8,128)(2,1)} copy(bf16[6,128,4096]{2,1,0:T(8,128)(2,1)} %attention_block.1) | data formatting | bytes 12582912
  (1 shorter events, 0.0 us)
